TPU v7x, 16 devices: a whole 2x2x2 slice. The times are simulated.
16 devices in a mesh: data: 16 (over z, y, x, core).
Axes of the slice: x: 2, y: 2, z: 2, core: 2. Of those that a mesh axis runs over, the one named last changes fastest.
Arguments:
- feat_img: bfloat16 [16384, 768], P('data')
- feat_txt: bfloat16 [16384, 768], P('data')
- w_img: bfloat16 [768, 768], replicated
- w_txt: bfloat16 [768, 768], replicated
- log_temp: float32 [], replicated
- logit_bias: float32 [], replicated
- pair_ids: int32 [16384], P('data')
Outputs:
- output 1: float32 [], replicated
- output 2: float32 [], replicated
- output 3: float32 [], replicated
- output 4: float32 [768, 768], replicated
- output 5: float32 [768, 768], replicated
All inputs are finite; a program needn't handle non-finite values.
Results may differ from a plain program's by a relative error of at most 0.001.
Values are sent between devices in bfloat16 or wider.
A program may use at most 1 GiB of HBM per device.

v0:
```python
import jax
import jax.numpy as jnp
from jax import lax
from jax.sharding import PartitionSpec as P

CONTRACT_ROWS = (((0,), (0,)), ((), ()))
CONTRACT_COLS = (((1,), (1,)), ((), ()))


def embed_rows(feat_rows, weights):
    raw_emb = jnp.dot(feat_rows, weights, preferred_element_type=jnp.float32)
    inv_norm = lax.rsqrt(jnp.sum(raw_emb * raw_emb, axis=1, keepdims=True))
    unit_emb = raw_emb * inv_norm
    return unit_emb, inv_norm, unit_emb.astype(jnp.bfloat16)


def weight_grad(feat_rows, unit_emb, inv_norm, grad_emb):
    raw_grad = inv_norm * (grad_emb - unit_emb * jnp.sum(unit_emb * grad_emb, axis=1, keepdims=True))
    return lax.dot_general(feat_rows, raw_grad.astype(jnp.bfloat16), CONTRACT_ROWS, preferred_element_type=jnp.float32)


def tile_terms(emb_img, ids_img, emb_txt, ids_txt, temp_scale, logit_bias, total_rows):
    sim_tile = lax.dot_general(emb_img, emb_txt, CONTRACT_COLS, preferred_element_type=jnp.float32)
    label_sign = jnp.where(ids_img[:, None] == ids_txt[None, :], 1.0, -1.0).astype(jnp.float32)
    margin = -label_sign * (temp_scale * sim_tile + logit_bias)
    grad_tile = -label_sign * jax.nn.sigmoid(margin) / total_rows
    grad_bf = grad_tile.astype(jnp.bfloat16)
    part_img = jnp.dot(grad_bf, emb_txt, preferred_element_type=jnp.float32)
    part_txt = lax.dot_general(grad_bf, emb_img, CONTRACT_ROWS, preferred_element_type=jnp.float32)
    loss_part = jnp.sum(jax.nn.softplus(margin))
    return part_img, part_txt, loss_part, jnp.sum(grad_tile * sim_tile), jnp.sum(grad_tile)


def solution(mesh):
    n_dev = mesh.shape["data"]
    next_perm = [(src_dev, (src_dev + 1) % n_dev) for src_dev in range(n_dev)]

    def local_fn(feat_img, feat_txt, w_img, w_txt, log_temp, logit_bias, pair_ids):
        total_rows = feat_img.shape[0] * n_dev
        temp_scale = jnp.exp(log_temp)
        unit_img, inv_img, emb_img = embed_rows(feat_img, w_img)
        unit_txt, inv_txt, emb_txt = embed_rows(feat_txt, w_txt)

        def visit_block(hop_index, loop_state):
            txt_blk, ids_blk, acc_txt, acc_img, loss_sum, temp_sum, bias_sum = loop_state
            part_img, part_txt, loss_part, temp_part, bias_part = tile_terms(
                emb_img, pair_ids, txt_blk, ids_blk, temp_scale, logit_bias, total_rows)
            txt_blk, ids_blk, acc_txt = lax.ppermute((txt_blk, ids_blk, acc_txt + part_txt), "data", next_perm)
            return (txt_blk, ids_blk, acc_txt, acc_img + part_img,
                    loss_sum + loss_part, temp_sum + temp_part, bias_sum + bias_part)

        zero_rows = jnp.zeros(emb_img.shape, jnp.float32)
        zero_sum = jnp.zeros((), jnp.float32)
        loop_state = (emb_txt, pair_ids, zero_rows, zero_rows, zero_sum, zero_sum, zero_sum)
        loop_state = lax.fori_loop(0, n_dev - 1, visit_block, loop_state)
        txt_blk, ids_blk, acc_txt, acc_img, loss_sum, temp_sum, bias_sum = loop_state
        part_img, part_txt, loss_part, temp_part, bias_part = tile_terms(
            emb_img, pair_ids, txt_blk, ids_blk, temp_scale, logit_bias, total_rows)
        home_txt = lax.ppermute(acc_txt + part_txt, "data", next_perm)
        grad_img = temp_scale * (acc_img + part_img)
        grad_txt = temp_scale * home_txt
        dw_img = weight_grad(feat_img, unit_img, inv_img, grad_img)
        dw_txt = weight_grad(feat_txt, unit_txt, inv_txt, grad_txt)
        totals = lax.psum((loss_sum + loss_part, temp_sum + temp_part, bias_sum + bias_part, dw_img, dw_txt), "data")
        return totals[0] / total_rows, temp_scale * totals[1], totals[2], totals[3], totals[4]

    return jax.shard_map(
        local_fn,
        mesh=mesh,
        in_specs=(P("data", None), P("data", None), P(None, None), P(None, None), P(), P(), P("data")),
        out_specs=(P(), P(), P(), P(None, None), P(None, None)),
        check_vma=False,
    )
```

profile of v0, /device:TPU:1, one launch (start us, length us, event | category | flops | bytes accessed | tf_op | source)
XLA Modules:
  0.0 1272.5 jit_solution(6890823804521030159)
XLA Ops:
  26.5 1060.4 %while.23 = (s32[]{:T(128)}, bf16[1024,768]{1,0:T(8,128)(2,1)S(1)}, s32[1024]{0:T(1024)S(1)}, f32[1024,768]{1,0:T(8,128)}, f32[1024,768]{1,0:T(8,128)}, /*index=...) while((s32[]{:T(128)}, bf16[1024,768]{1,0:T(8,128)(2,1)S(1)}, ...), condition=%wide.region_6.7_spmd.clone, body=%wide.region_2.6_spmd.clone.sunk | while | flops 4857266176 | bytes 61899124 | solution.py:55
  28.5 8.8 fusion.44
  55.1 42.2 %collective-permute-done.1 = s32[1024]{0:T(1024)S(1)} collective-permute-done((s32[1024]{0:T(1024)S(1)}, s32[1024]{0:T(1024)S(1)}, u32[]{:S(2)}, u32[]{:S(2)}) %collective-permute-start.1) | collective-permute-done | bytes 4128 | tf_op jit(solution)/shard_map/while/body/eval_jaxpr/ppermute | solution.py:48
  127.6 40.4 %collective-permute-done.1 = s32[1024]{0:T(1024)S(1)} collective-permute-done((s32[1024]{0:T(1024)S(1)}, s32[1024]{0:T(1024)S(1)}, u32[]{:S(2)}, u32[]{:S(2)}) %collective-permute-start.1) | collective-permute-done | bytes 4128 | tf_op jit(solution)/shard_map/while/body/eval_jaxpr/ppermute | solution.py:48
  199.2 39.5 %collective-permute-done.1 = s32[1024]{0:T(1024)S(1)} collective-permute-done((s32[1024]{0:T(1024)S(1)}, s32[1024]{0:T(1024)S(1)}, u32[]{:S(2)}, u32[]{:S(2)}) %collective-permute-start.1) | collective-permute-done | bytes 4128 | tf_op jit(solution)/shard_map/while/body/eval_jaxpr/ppermute | solution.py:48
  240.7 8.8 fusion.44
  270.8 38.6 %collective-permute-done.1 = s32[1024]{0:T(1024)S(1)} collective-permute-done((s32[1024]{0:T(1024)S(1)}, s32[1024]{0:T(1024)S(1)}, u32[]{:S(2)}, u32[]{:S(2)}) %collective-permute-start.1) | collective-permute-done | bytes 4128 | tf_op jit(solution)/shard_map/while/body/eval_jaxpr/ppermute | solution.py:48
  342.4 37.7 %collective-permute-done.1 = s32[1024]{0:T(1024)S(1)} collective-permute-done((s32[1024]{0:T(1024)S(1)}, s32[1024]{0:T(1024)S(1)}, u32[]{:S(2)}, u32[]{:S(2)}) %collective-permute-start.1) | collective-permute-done | bytes 4128 | tf_op jit(solution)/shard_map/while/body/eval_jaxpr/ppermute | solution.py:48
  413.9 36.8 %collective-permute-done.1 = s32[1024]{0:T(1024)S(1)} collective-permute-done((s32[1024]{0:T(1024)S(1)}, s32[1024]{0:T(1024)S(1)}, u32[]{:S(2)}, u32[]{:S(2)}) %collective-permute-start.1) | collective-permute-done | bytes 4128 | tf_op jit(solution)/shard_map/while/body/eval_jaxpr/ppermute | solution.py:48
  485.5 35.9 %collective-permute-done.1 = s32[1024]{0:T(1024)S(1)} collective-permute-done((s32[1024]{0:T(1024)S(1)}, s32[1024]{0:T(1024)S(1)}, u32[]{:S(2)}, u32[]{:S(2)}) %collective-permute-start.1) | collective-permute-done | bytes 4128 | tf_op jit(solution)/shard_map/while/body/eval_jaxpr/ppermute | solution.py:48
  557.1 35.0 %collective-permute-done.1 = s32[1024]{0:T(1024)S(1)} collective-permute-done((s32[1024]{0:T(1024)S(1)}, s32[1024]{0:T(1024)S(1)}, u32[]{:S(2)}, u32[]{:S(2)}) %collective-permute-start.1) | collective-permute-done | bytes 4128 | tf_op jit(solution)/shard_map/while/body/eval_jaxpr/ppermute | solution.py:48
  628.7 34.1 %collective-permute-done.1 = s32[1024]{0:T(1024)S(1)} collective-permute-done((s32[1024]{0:T(1024)S(1)}, s32[1024]{0:T(1024)S(1)}, u32[]{:S(2)}, u32[]{:S(2)}) %collective-permute-start.1) | collective-permute-done | bytes 4128 | tf_op jit(solution)/shard_map/while/body/eval_jaxpr/ppermute | solution.py:48
  700.3 33.2 %collective-permute-done.1 = s32[1024]{0:T(1024)S(1)} collective-permute-done((s32[1024]{0:T(1024)S(1)}, s32[1024]{0:T(1024)S(1)}, u32[]{:S(2)}, u32[]{:S(2)}) %collective-permute-start.1) | collective-permute-done | bytes 4128 | tf_op jit(solution)/shard_map/while/body/eval_jaxpr/ppermute | solution.py:48
  771.8 32.3 %collective-permute-done.1 = s32[1024]{0:T(1024)S(1)} collective-permute-done((s32[1024]{0:T(1024)S(1)}, s32[1024]{0:T(1024)S(1)}, u32[]{:S(2)}, u32[]{:S(2)}) %collective-permute-start.1) | collective-permute-done | bytes 4128 | tf_op jit(solution)/shard_map/while/body/eval_jaxpr/ppermute | solution.py:48
  843.4 31.4 %collective-permute-done.1 = s32[1024]{0:T(1024)S(1)} collective-permute-done((s32[1024]{0:T(1024)S(1)}, s32[1024]{0:T(1024)S(1)}, u32[]{:S(2)}, u32[]{:S(2)}) %collective-permute-start.1) | collective-permute-done | bytes 4128 | tf_op jit(solution)/shard_map/while/body/eval_jaxpr/ppermute | solution.py:48
  894.5 8.9 collective-permute-start
  915.0 30.5 %collective-permute-done.1 = s32[1024]{0:T(1024)S(1)} collective-permute-done((s32[1024]{0:T(1024)S(1)}, s32[1024]{0:T(1024)S(1)}, u32[]{:S(2)}, u32[]{:S(2)}) %collective-permute-start.1) | collective-permute-done | bytes 4128 | tf_op jit(solution)/shard_map/while/body/eval_jaxpr/ppermute | solution.py:48
  965.1 9.8 collective-permute-start
  986.6 29.7 %collective-permute-done.1 = s32[1024]{0:T(1024)S(1)} collective-permute-done((s32[1024]{0:T(1024)S(1)}, s32[1024]{0:T(1024)S(1)}, u32[]{:S(2)}, u32[]{:S(2)}) %collective-permute-start.1) | collective-permute-done | bytes 4128 | tf_op jit(solution)/shard_map/while/body/eval_jaxpr/ppermute | solution.py:48
  1035.8 10.7 collective-permute-start
  1058.2 28.8 %collective-permute-done.1 = s32[1024]{0:T(1024)S(1)} collective-permute-done((s32[1024]{0:T(1024)S(1)}, s32[1024]{0:T(1024)S(1)}, u32[]{:S(2)}, u32[]{:S(2)}) %collective-permute-start.1) | collective-permute-done | bytes 4128 | tf_op jit(solution)/shard_map/while/body/eval_jaxpr/ppermute | solution.py:48
  1117.0 21.7 %collective-permute-done.3 = f32[1024,768]{0,1:T(8,128)} collective-permute-done((f32[1024,768]{0,1:T(8,128)}, f32[1024,768]{0,1:T(8,128)}, u32[]{:S(2)}, u32[]{:S(2)}) %collective-permute-start.3) | collective-permute-done | bytes 3145760 | tf_op jit(solution)/shard_map/ppermute | solution.py:59
  1148.0 61.1 %all-reduce = (f32[]{:T(128)}, f32[]{:T(128)}, f32[]{:T(128)}) all-reduce(f32[]{:T(128)S(6)} %add.71, f32[]{:T(128)S(6)} %add.73, f32[]{:T(128)S(6)} %add.74), channel_id=1, replica_groups=mesh['data'=16] {'data'}, use_global_device_ids=true, to_apply=%region_8.9 | all-reduce | flops 3 | bytes 24 | tf_op jit(solution)/shard_map/psum | solution.py:64
  1210.5 46.8 %all-reduce.4.cloned.1.call-done = (f32[768,768]{0,1:T(8,128)}, f32[768,768]{0,1:T(8,128)}) async-done(((f32[768,768]{0,1:T(8,128)}, f32[768,768]{0,1:T(8,128)}), (f32[768,768]{0,1:T(8,128)}, f32[768,768]{0,1:T(8,128)})) %all-reduce.4.cloned.1.call-update) | async-done | bytes 4718608 | tf_op jit(solution)/shard_map/psum | solution.py:64
  (255 shorter events, 521.6 us)
Async XLA Ops:
  7.2 1250.1 %all-reduce.4.cloned.1.call-start = ((), (), s32[]{:S(2)}) async-start(), calls=%async_computation | async-start | bytes 9437184 | tf_op jit(solution)/shard_map/psum | solution.py:64
  43.6 53.7 %collective-permute-start.2 = (f32[1024,768]{1,0:T(8,128)}, f32[1024,768]{1,0:T(8,128)}, u32[]{:S(2)}, u32[]{:S(2)}) collective-permute-start(f32[1024,768]{1,0:T(8,128)} %convolution_add_fusion.3), channel_id=1, source_target_pairs={{0,1},{1,2},{2,3},{3,4},{4,5},{5,6},{6,7},{7,8},{8,9},{9,10},{10,1... | collective-permute-start | bytes 9437192 | tf_op jit(solution)/shard_map/while/body/eval_jaxpr/ppermute | solution.py:48
  46.2 51.1 %collective-permute-start = (bf16[1024,768]{1,0:T(8,128)(2,1)}, bf16[1024,768]{1,0:T(8,128)(2,1)S(1)}, u32[]{:S(2)}, u32[]{:S(2)}) collective-permute-start(bf16[1024,768]{1,0:T(8,128)(2,1)} %copy.29), channel_id=1, source_target_pairs={{0,1},{1,2},{2,3},{3,4},{4,5},{5,6},{6,7},{7,8},{8,9},{9,10},{10,1... | collective-permute-start | bytes 4718600 | tf_op jit(solution)/shard_map/while/body/eval_jaxpr/ppermute | solution.py:48
  114.4 53.6 %collective-permute-start.2 = (f32[1024,768]{1,0:T(8,128)}, f32[1024,768]{1,0:T(8,128)}, u32[]{:S(2)}, u32[]{:S(2)}) collective-permute-start(f32[1024,768]{1,0:T(8,128)} %convolution_add_fusion.3), channel_id=1, source_target_pairs={{0,1},{1,2},{2,3},{3,4},{4,5},{5,6},{6,7},{7,8},{8,9},{9,10},{10,1... | collective-permute-start | bytes 9437192 | tf_op jit(solution)/shard_map/while/body/eval_jaxpr/ppermute | solution.py:48
  116.9 51.1 %collective-permute-start = (bf16[1024,768]{1,0:T(8,128)(2,1)}, bf16[1024,768]{1,0:T(8,128)(2,1)S(1)}, u32[]{:S(2)}, u32[]{:S(2)}) collective-permute-start(bf16[1024,768]{1,0:T(8,128)(2,1)} %copy.29), channel_id=1, source_target_pairs={{0,1},{1,2},{2,3},{3,4},{4,5},{5,6},{6,7},{7,8},{8,9},{9,10},{10,1... | collective-permute-start | bytes 4718600 | tf_op jit(solution)/shard_map/while/body/eval_jaxpr/ppermute | solution.py:48
  185.1 53.6 %collective-permute-start.2 = (f32[1024,768]{1,0:T(8,128)}, f32[1024,768]{1,0:T(8,128)}, u32[]{:S(2)}, u32[]{:S(2)}) collective-permute-start(f32[1024,768]{1,0:T(8,128)} %convolution_add_fusion.3), channel_id=1, source_target_pairs={{0,1},{1,2},{2,3},{3,4},{4,5},{5,6},{6,7},{7,8},{8,9},{9,10},{10,1... | collective-permute-start | bytes 9437192 | tf_op jit(solution)/shard_map/while/body/eval_jaxpr/ppermute | solution.py:48
  187.6 51.1 %collective-permute-start = (bf16[1024,768]{1,0:T(8,128)(2,1)}, bf16[1024,768]{1,0:T(8,128)(2,1)S(1)}, u32[]{:S(2)}, u32[]{:S(2)}) collective-permute-start(bf16[1024,768]{1,0:T(8,128)(2,1)} %copy.29), channel_id=1, source_target_pairs={{0,1},{1,2},{2,3},{3,4},{4,5},{5,6},{6,7},{7,8},{8,9},{9,10},{10,1... | collective-permute-start | bytes 4718600 | tf_op jit(solution)/shard_map/while/body/eval_jaxpr/ppermute | solution.py:48
  255.8 53.6 %collective-permute-start.2 = (f32[1024,768]{1,0:T(8,128)}, f32[1024,768]{1,0:T(8,128)}, u32[]{:S(2)}, u32[]{:S(2)}) collective-permute-start(f32[1024,768]{1,0:T(8,128)} %convolution_add_fusion.3), channel_id=1, source_target_pairs={{0,1},{1,2},{2,3},{3,4},{4,5},{5,6},{6,7},{7,8},{8,9},{9,10},{10,1... | collective-permute-start | bytes 9437192 | tf_op jit(solution)/shard_map/while/body/eval_jaxpr/ppermute | solution.py:48
  258.3 51.1 %collective-permute-start = (bf16[1024,768]{1,0:T(8,128)(2,1)}, bf16[1024,768]{1,0:T(8,128)(2,1)S(1)}, u32[]{:S(2)}, u32[]{:S(2)}) collective-permute-start(bf16[1024,768]{1,0:T(8,128)(2,1)} %copy.29), channel_id=1, source_target_pairs={{0,1},{1,2},{2,3},{3,4},{4,5},{5,6},{6,7},{7,8},{8,9},{9,10},{10,1... | collective-permute-start | bytes 4718600 | tf_op jit(solution)/shard_map/while/body/eval_jaxpr/ppermute | solution.py:48
  326.5 53.6 %collective-permute-start.2 = (f32[1024,768]{1,0:T(8,128)}, f32[1024,768]{1,0:T(8,128)}, u32[]{:S(2)}, u32[]{:S(2)}) collective-permute-start(f32[1024,768]{1,0:T(8,128)} %convolution_add_fusion.3), channel_id=1, source_target_pairs={{0,1},{1,2},{2,3},{3,4},{4,5},{5,6},{6,7},{7,8},{8,9},{9,10},{10,1... | collective-permute-start | bytes 9437192 | tf_op jit(solution)/shard_map/while/body/eval_jaxpr/ppermute | solution.py:48
  329.0 51.1 %collective-permute-start = (bf16[1024,768]{1,0:T(8,128)(2,1)}, bf16[1024,768]{1,0:T(8,128)(2,1)S(1)}, u32[]{:S(2)}, u32[]{:S(2)}) collective-permute-start(bf16[1024,768]{1,0:T(8,128)(2,1)} %copy.29), channel_id=1, source_target_pairs={{0,1},{1,2},{2,3},{3,4},{4,5},{5,6},{6,7},{7,8},{8,9},{9,10},{10,1... | collective-permute-start | bytes 4718600 | tf_op jit(solution)/shard_map/while/body/eval_jaxpr/ppermute | solution.py:48
  397.1 53.6 %collective-permute-start.2 = (f32[1024,768]{1,0:T(8,128)}, f32[1024,768]{1,0:T(8,128)}, u32[]{:S(2)}, u32[]{:S(2)}) collective-permute-start(f32[1024,768]{1,0:T(8,128)} %convolution_add_fusion.3), channel_id=1, source_target_pairs={{0,1},{1,2},{2,3},{3,4},{4,5},{5,6},{6,7},{7,8},{8,9},{9,10},{10,1... | collective-permute-start | bytes 9437192 | tf_op jit(solution)/shard_map/while/body/eval_jaxpr/ppermute | solution.py:48
  399.6 51.1 %collective-permute-start = (bf16[1024,768]{1,0:T(8,128)(2,1)}, bf16[1024,768]{1,0:T(8,128)(2,1)S(1)}, u32[]{:S(2)}, u32[]{:S(2)}) collective-permute-start(bf16[1024,768]{1,0:T(8,128)(2,1)} %copy.29), channel_id=1, source_target_pairs={{0,1},{1,2},{2,3},{3,4},{4,5},{5,6},{6,7},{7,8},{8,9},{9,10},{10,1... | collective-permute-start | bytes 4718600 | tf_op jit(solution)/shard_map/while/body/eval_jaxpr/ppermute | solution.py:48
  467.8 53.6 %collective-permute-start.2 = (f32[1024,768]{1,0:T(8,128)}, f32[1024,768]{1,0:T(8,128)}, u32[]{:S(2)}, u32[]{:S(2)}) collective-permute-start(f32[1024,768]{1,0:T(8,128)} %convolution_add_fusion.3), channel_id=1, source_target_pairs={{0,1},{1,2},{2,3},{3,4},{4,5},{5,6},{6,7},{7,8},{8,9},{9,10},{10,1... | collective-permute-start | bytes 9437192 | tf_op jit(solution)/shard_map/while/body/eval_jaxpr/ppermute | solution.py:48
  538.5 53.6 %collective-permute-start.2 = (f32[1024,768]{1,0:T(8,128)}, f32[1024,768]{1,0:T(8,128)}, u32[]{:S(2)}, u32[]{:S(2)}) collective-permute-start(f32[1024,768]{1,0:T(8,128)} %convolution_add_fusion.3), channel_id=1, source_target_pairs={{0,1},{1,2},{2,3},{3,4},{4,5},{5,6},{6,7},{7,8},{8,9},{9,10},{10,1... | collective-permute-start | bytes 9437192 | tf_op jit(solution)/shard_map/while/body/eval_jaxpr/ppermute | solution.py:48
  609.2 53.6 %collective-permute-start.2 = (f32[1024,768]{1,0:T(8,128)}, f32[1024,768]{1,0:T(8,128)}, u32[]{:S(2)}, u32[]{:S(2)}) collective-permute-start(f32[1024,768]{1,0:T(8,128)} %convolution_add_fusion.3), channel_id=1, source_target_pairs={{0,1},{1,2},{2,3},{3,4},{4,5},{5,6},{6,7},{7,8},{8,9},{9,10},{10,1... | collective-permute-start | bytes 9437192 | tf_op jit(solution)/shard_map/while/body/eval_jaxpr/ppermute | solution.py:48
  679.9 53.6 %collective-permute-start.2 = (f32[1024,768]{1,0:T(8,128)}, f32[1024,768]{1,0:T(8,128)}, u32[]{:S(2)}, u32[]{:S(2)}) collective-permute-start(f32[1024,768]{1,0:T(8,128)} %convolution_add_fusion.3), channel_id=1, source_target_pairs={{0,1},{1,2},{2,3},{3,4},{4,5},{5,6},{6,7},{7,8},{8,9},{9,10},{10,1... | collective-permute-start | bytes 9437192 | tf_op jit(solution)/shard_map/while/body/eval_jaxpr/ppermute | solution.py:48
  682.4 51.1 %collective-permute-start = (bf16[1024,768]{1,0:T(8,128)(2,1)}, bf16[1024,768]{1,0:T(8,128)(2,1)S(1)}, u32[]{:S(2)}, u32[]{:S(2)}) collective-permute-start(bf16[1024,768]{1,0:T(8,128)(2,1)} %copy.29), channel_id=1, source_target_pairs={{0,1},{1,2},{2,3},{3,4},{4,5},{5,6},{6,7},{7,8},{8,9},{9,10},{10,1... | collective-permute-start | bytes 4718600 | tf_op jit(solution)/shard_map/while/body/eval_jaxpr/ppermute | solution.py:48
  750.6 53.6 %collective-permute-start.2 = (f32[1024,768]{1,0:T(8,128)}, f32[1024,768]{1,0:T(8,128)}, u32[]{:S(2)}, u32[]{:S(2)}) collective-permute-start(f32[1024,768]{1,0:T(8,128)} %convolution_add_fusion.3), channel_id=1, source_target_pairs={{0,1},{1,2},{2,3},{3,4},{4,5},{5,6},{6,7},{7,8},{8,9},{9,10},{10,1... | collective-permute-start | bytes 9437192 | tf_op jit(solution)/shard_map/while/body/eval_jaxpr/ppermute | solution.py:48
  821.3 53.6 %collective-permute-start.2 = (f32[1024,768]{1,0:T(8,128)}, f32[1024,768]{1,0:T(8,128)}, u32[]{:S(2)}, u32[]{:S(2)}) collective-permute-start(f32[1024,768]{1,0:T(8,128)} %convolution_add_fusion.3), channel_id=1, source_target_pairs={{0,1},{1,2},{2,3},{3,4},{4,5},{5,6},{6,7},{7,8},{8,9},{9,10},{10,1... | collective-permute-start | bytes 9437192 | tf_op jit(solution)/shard_map/while/body/eval_jaxpr/ppermute | solution.py:48
  891.9 53.6 %collective-permute-start.2 = (f32[1024,768]{1,0:T(8,128)}, f32[1024,768]{1,0:T(8,128)}, u32[]{:S(2)}, u32[]{:S(2)}) collective-permute-start(f32[1024,768]{1,0:T(8,128)} %convolution_add_fusion.3), channel_id=1, source_target_pairs={{0,1},{1,2},{2,3},{3,4},{4,5},{5,6},{6,7},{7,8},{8,9},{9,10},{10,1... | collective-permute-start | bytes 9437192 | tf_op jit(solution)/shard_map/while/body/eval_jaxpr/ppermute | solution.py:48
  962.6 53.6 %collective-permute-start.2 = (f32[1024,768]{1,0:T(8,128)}, f32[1024,768]{1,0:T(8,128)}, u32[]{:S(2)}, u32[]{:S(2)}) collective-permute-start(f32[1024,768]{1,0:T(8,128)} %convolution_add_fusion.3), channel_id=1, source_target_pairs={{0,1},{1,2},{2,3},{3,4},{4,5},{5,6},{6,7},{7,8},{8,9},{9,10},{10,1... | collective-permute-start | bytes 9437192 | tf_op jit(solution)/shard_map/while/body/eval_jaxpr/ppermute | solution.py:48
  1033.3 53.6 %collective-permute-start.2 = (f32[1024,768]{1,0:T(8,128)}, f32[1024,768]{1,0:T(8,128)}, u32[]{:S(2)}, u32[]{:S(2)}) collective-permute-start(f32[1024,768]{1,0:T(8,128)} %convolution_add_fusion.3), channel_id=1, source_target_pairs={{0,1},{1,2},{2,3},{3,4},{4,5},{5,6},{6,7},{7,8},{8,9},{9,10},{10,1... | collective-permute-start | bytes 9437192 | tf_op jit(solution)/shard_map/while/body/eval_jaxpr/ppermute | solution.py:48
  1035.8 51.1 %collective-permute-start = (bf16[1024,768]{1,0:T(8,128)(2,1)}, bf16[1024,768]{1,0:T(8,128)(2,1)S(1)}, u32[]{:S(2)}, u32[]{:S(2)}) collective-permute-start(bf16[1024,768]{1,0:T(8,128)(2,1)} %copy.29), channel_id=1, source_target_pairs={{0,1},{1,2},{2,3},{3,4},{4,5},{5,6},{6,7},{7,8},{8,9},{9,10},{10,1... | collective-permute-start | bytes 4718600 | tf_op jit(solution)/shard_map/while/body/eval_jaxpr/ppermute | solution.py:48
  (66 other events, 1329.3 us)
Sparse Core Ops, SparseCore 0:
  1146.4 110.8 all-reduce.3
where the time goes:
time: 1280 us; the launch traced here: 1270 us
  waiting for transfers between devices  595 us (46%)
  matrix products  353 us (28%)
  starting transfers between devices  158 us (12%)
  blocking collectives  61.1 us (5%)
  local copies, waits for them, and re-layouts  52.9 us (4%)
  loops' own time  27.1 us (2%)
  between operations  20.9 us (2%)
    ppermute x45, waiting for transfers between devices, visit_block(): lax.ppermute((txt_blk, ids_blk, acc_txt + part_txt), 'data', next_perm)  526 us
    ppermute x45, starting transfers between devices, visit_block(): lax.ppermute((txt_blk, ids_blk, acc_txt + part_txt), 'data', next_perm)  156 us
    dot_general x16, matrix products, tile_terms(): lax.dot_general(emb_img, emb_txt, CONTRACT_COLS, preferred_element_type=j...  140 us
    dot_general x16, matrix products, tile_terms(): part_img = jnp.dot(grad_bf, emb_txt, preferred_element_type=jnp.float32)  101 us
    dot_general x16, matrix products, tile_terms(): lax.dot_general(grad_bf, emb_img, CONTRACT_ROWS, preferred_element_type=j...  97.6 us
    psum x1, blocking collectives, local_fn(): lax.psum((loss_sum + loss_part, temp_sum + temp_part, bias_sum + bias_par...  61.1 us
    psum x1, waiting for transfers between devices, local_fn(): lax.psum((loss_sum + loss_part, temp_sum + temp_part, bias_sum + bias_par...  46.8 us
    while x90, local copies, waits for them, and re-layouts  29.7 us
  transfers between devices with their start and end apart: 47, of which 17 were waited for; matrix products, arithmetic and copies ran while one was open for 8% of the time, Pallas kernels for 0%

commit v1 on v0

v1 whole, which is shorter than its diff:
```python
import jax
import jax.numpy as jnp
from jax import lax
from jax.experimental import pallas as pl
from jax.experimental.pallas import tpu as pltpu
from jax.sharding import PartitionSpec as P

F32, BF16 = jnp.float32, jnp.bfloat16
MESH = pl.DeviceIdType.MESH
ROWS, EMBED = 1024, 768
TILE_M, CHUNK_R = 512, 16
LOG2E = 1.4426950408889634
CONTRACT_ROWS = (((0,), (0,)), ((), ()))
CONTRACT_COLS = (((1,), (1,)), ((), ()))

SLOT = {0: 0, 1: 2, 2: 3, 4: 4, 3: 5, 6: 6, 5: 7, 7: 8}
PART_ROWS = ((0, 352), (352, 336), (688, 336))
PART_DIMS = ((1, 2, 4), (2, 4, 1), (4, 1, 2))


def embed_rows(feat_rows, weights):
    raw_emb = jnp.dot(feat_rows, weights, preferred_element_type=F32)
    inv_norm = lax.rsqrt(jnp.sum(raw_emb * raw_emb, axis=1, keepdims=True))
    unit_emb = raw_emb * inv_norm
    return unit_emb, inv_norm, unit_emb.astype(BF16)


def weight_grad(feat_rows, unit_emb, inv_norm, grad_emb):
    raw_grad = inv_norm * (grad_emb - unit_emb * jnp.sum(unit_emb * grad_emb, axis=1, keepdims=True))
    return lax.dot_general(feat_rows, raw_grad.astype(BF16), CONTRACT_ROWS, preferred_element_type=F32)


def gather_plan():
    own = [(p, 0, PART_DIMS[p][k]) for k in range(3) for p in range(3)]
    first, last = [], []
    for p, (d1, d2, d3) in enumerate(PART_DIMS):
        first.append((p, d1, d2))
    for p, (d1, d2, d3) in enumerate(PART_DIMS):
        first.append((p, d1, d3))
    for p, (d1, d2, d3) in enumerate(PART_DIMS):
        first.append((p, d2, d3))
    for p, (d1, d2, d3) in enumerate(PART_DIMS):
        last.append((p, d1 | d2, d3))
    return own, first, last


def pair_kernel(scal_ref, img_ref, txt_ref, ids_ref, idrow_ref, dimg_ref, dtxt_ref, sums_ref,
                slots, ids_all, id_rows, acc, partner, s0, s1, g0, g1, sums,
                send_sem, recv_sem, ids_send, ids_recv, pair_send, pair_recv, grad_send, grad_recv, load_sem):
    me = lax.axis_index("data")
    core = me % 2
    chip = me // 2

    def peer(rel):
        where = chip
        for d in (1, 2, 4):
            if rel & d:
                where = where + d * (1 - 2 * ((chip // d) % 2))
        return where * 2 + core

    other_core = chip * 2 + (1 - core)
    loads = [pltpu.make_async_copy(src, slots.at[a, 0], load_sem.at[a]) for a, src in ((0, txt_ref), (1, img_ref))]
    for c in loads:
        c.start()
    id_load = pltpu.make_async_copy(ids_ref, ids_all.at[0], load_sem.at[2])
    id_load.start()
    loads.append(pltpu.make_async_copy(idrow_ref, id_rows.at[pl.ds(0, ROWS)], load_sem.at[3]))
    loads[2].start()

    barrier = pltpu.get_barrier_semaphore()
    partners = [other_core] + [peer(rel) for rel in range(1, 8)]
    for dev in partners:
        pl.semaphore_signal(barrier, inc=1, device_id=(dev,), device_id_type=MESH)
    acc[...] = jnp.zeros_like(acc)
    sums[...] = jnp.zeros_like(sums)
    pl.semaphore_wait(barrier, len(partners))

    def part_copy(a, p, rel, d):
        lo, size = PART_ROWS[p]
        return pltpu.make_async_remote_copy(
            src_ref=slots.at[a, SLOT[rel], pl.ds(lo, size)],
            dst_ref=slots.at[a, SLOT[rel ^ d], pl.ds(lo, size)],
            send_sem=send_sem.at[a, p, SLOT[rel ^ d]],
            recv_sem=recv_sem.at[a, p, SLOT[rel ^ d]],
            device_id=(peer(d),), device_id_type=MESH)

    def arrival(a, p, rel):
        d = next(x for x in reversed(PART_DIMS[p]) if rel & x)
        part_copy(a, p, rel ^ d, d).wait_recv()

    own, first, last = gather_plan()
    pair_copies = [pltpu.make_async_remote_copy(
        src_ref=slots.at[a, 0], dst_ref=slots.at[a, 1], send_sem=pair_send.at[a], recv_sem=pair_recv.at[a],
        device_id=(other_core,), device_id_type=MESH) for a in range(2)]
    pair_copies.append(pltpu.make_async_remote_copy(
        src_ref=id_rows.at[pl.ds(0, ROWS)], dst_ref=id_rows.at[pl.ds(ROWS, ROWS)], send_sem=pair_send.at[2],
        recv_sem=pair_recv.at[2], device_id=(other_core,), device_id_type=MESH))
    id_copies = []
    for i, dev in enumerate(partners):
        rel_slot = 1 if i == 0 else SLOT[i]
        id_copies.append(pltpu.make_async_remote_copy(
            src_ref=ids_all.at[0], dst_ref=ids_all.at[rel_slot], send_sem=ids_send.at[rel_slot],
            recv_sem=ids_recv.at[rel_slot], device_id=(dev,), device_id_type=MESH))
    id_load.wait()
    for c in id_copies:
        c.start()
    for c in loads:
        c.wait()
    for c in pair_copies[::-1]:
        c.start()
    for send in own:
        part_copy(0, *send).start()

    scale, bias = scal_ref[0], scal_ref[1]
    for c in id_copies:
        c.wait_recv()
    for c in pair_copies:
        c.wait_recv()

    n_m = 2 * ROWS // TILE_M

    def slot_of(block):
        return block + (block + 7) // 8

    def scores(a, t, s_ref):
        m, slot = pl.multiple_of((t % n_m) * TILE_M, TILE_M), slot_of(t // n_m)
        rows = slots[1 - a, (t % n_m) // (n_m // 2), pl.ds(pl.multiple_of((t % (n_m // 2)) * TILE_M, TILE_M), TILE_M), :]
        s_ref[...] = lax.dot_general(rows, slots[a, slot], CONTRACT_COLS, preferred_element_type=F32)

    def tile_grad(a, t, s_ref, g_ref):
        m, slot = pl.multiple_of((t % n_m) * TILE_M, TILE_M), slot_of(t // n_m)

        col_ids = ids_all[slot]

        def rows_step(i, carry):
            x0, x1 = carry
            top = pl.multiple_of(i * CHUNK_R, CHUNK_R)
            row_ids = jnp.concatenate([id_rows[pl.ds(pl.multiple_of(m + top, CHUNK_R), CHUNK_R), :]] * 8, axis=1)
            sim = s_ref[pl.ds(top, CHUNK_R), :]
            sign = jnp.where(row_ids == col_ids, -1.0, 1.0)
            margin = sign * (scale * sim + bias)
            e = jnp.exp2(jnp.abs(margin) * (-LOG2E))
            d = 1.0 + e
            r = 1.0 / d
            grad = sign * jnp.where(margin >= 0, r, e * r)
            g_ref[pl.ds(top, CHUNK_R), :] = grad.astype(BF16)
            if a == 0:
                return x0 + jnp.maximum(margin, 0.0), x1 * d + e
            return x0 + grad * sim, x1 + grad

        x1 = jnp.zeros((CHUNK_R, ROWS), F32) if a == 0 else sums[3]
        x0, x1 = lax.fori_loop(0, TILE_M // CHUNK_R, rows_step, (sums[2 * a], x1), unroll=True)
        sums[2 * a] = x0
        sums[2 * a + 1] = sums[1] + jnp.log1p(x1) if a == 0 else x1

    def row_grad(a, t, g_ref):
        m, slot = pl.multiple_of((t % n_m) * TILE_M, TILE_M), slot_of(t // n_m)
        acc[1 - a, pl.ds(m, TILE_M), :] += jnp.dot(g_ref[...], slots[a, slot], preferred_element_type=F32)

    def block_needs(a, rel, seen):
        return [(a, p, rel) for p in range(3) if (a, p, rel) not in seen]

    order = sorted(SLOT, key=SLOT.get)
    seen = set()
    steps = {}

    def add(key, waits=(), sends=()):
        w = [x for x in dict.fromkeys(waits) if x not in seen]
        seen.update(w)
        steps.setdefault(key, []).append((w, list(sends)))

    def forwards(a, sends):
        return [(a, p, rel) for p, rel, _ in sends], [(a,) + s for s in sends]

    add((0, 1), *forwards(0, first))
    add((0, 1), block_needs(0, order[1], seen))
    add((0, 2), block_needs(0, order[2], seen))
    add((0, 2), *forwards(0, last))
    add((0, 2), (), [(1,) + s for s in own])
    for b in range(3, 8):
        add((0, b), block_needs(0, order[b], seen))
    add((0, 7), *forwards(1, first))
    add((1, 1), block_needs(1, order[1], seen))
    add((1, 2), block_needs(1, order[2], seen))
    add((1, 2), *forwards(1, last))
    for b in range(3, 8):
        add((1, b), block_needs(1, order[b], seen))

    def run_steps(key):
        for waits, sends in steps.get(key, ()):
            for w in waits:
                arrival(*w)
            for s in sends:
                part_copy(*s).start()

    def stream(a):
        t0, t_end = 0, 8 * n_m
        scores(a, t0, s0)
        scores(a, t0 + 1, s1)
        tile_grad(a, t0, s0, g0)

        def body(k, carry):
            t = t0 + 2 * k + 1
            for b in range(1, 8):
                @pl.when(t + 1 == b * n_m)
                def _():
                    run_steps((a, b))
            scores(a, t + 1, s0)
            tile_grad(a, t, s1, g1)
            row_grad(a, t - 1, g0)
            scores(a, t + 2, s1)
            tile_grad(a, t + 1, s0, g0)
            row_grad(a, t, g1)
            return carry

        lax.fori_loop(0, (t_end - t0 - 2) // 2, body, 0)
        tile_grad(a, t_end - 1, s1, g1)
        row_grad(a, t_end - 2, g0)
        row_grad(a, t_end - 1, g1)

    grad_copies = [pltpu.make_async_remote_copy(
        src_ref=acc.at[x, pl.ds(ROWS, ROWS)], dst_ref=partner.at[x], send_sem=grad_send.at[x],
        recv_sem=grad_recv.at[x], device_id=(other_core,), device_id_type=MESH) for x in range(2)]

    stream(0)
    grad_copies[1].start()
    stream(1)
    grad_copies[0].start()
    grad_copies[1].wait_recv()
    acc[1, 0:ROWS, :] += partner[1]
    outs = [pltpu.make_async_copy(acc.at[x, pl.ds(0, ROWS)], ref, load_sem.at[x]) for x, ref in ((1, dimg_ref), (0, dtxt_ref))]
    outs[0].start()
    sums_ref[...] = sums[...]
    grad_copies[0].wait_recv()
    acc[0, 0:ROWS, :] += partner[0]
    outs[1].start()
    for c in outs:
        c.wait()
    for c in grad_copies + pair_copies + id_copies:
        c.wait_send()
    for a in range(2):
        for send in own + first + last:
            part_copy(a, *send).wait_send()


def solution(mesh):
    n_dev = mesh.shape["data"]

    def local_fn(feat_img, feat_txt, w_img, w_txt, log_temp, logit_bias, pair_ids):
        total_rows = feat_img.shape[0] * n_dev
        temp_scale = jnp.exp(log_temp)
        unit_img, inv_img, emb_img = embed_rows(feat_img, w_img)
        unit_txt, inv_txt, emb_txt = embed_rows(feat_txt, w_txt)
        vmem = pl.BlockSpec(memory_space=pltpu.VMEM)
        hbm = pl.BlockSpec(memory_space=pl.ANY)
        dma = pltpu.SemaphoreType.DMA
        part_img, part_txt, sums = pl.pallas_call(
            pair_kernel,
            out_shape=[jax.ShapeDtypeStruct((ROWS, EMBED), F32)] * 2 + [jax.ShapeDtypeStruct((4, CHUNK_R, ROWS), F32)],
            in_specs=[pl.BlockSpec(memory_space=pltpu.SMEM), hbm, hbm, hbm, hbm],
            out_specs=[hbm, hbm, vmem],
            scratch_shapes=[
                pltpu.VMEM((2, 9, ROWS, EMBED), BF16),
                pltpu.VMEM((9, 1, ROWS), jnp.int32),
                pltpu.VMEM((2 * ROWS, 128), jnp.int32),
                pltpu.VMEM((2, 2 * ROWS, EMBED), F32),
                pltpu.VMEM((2, ROWS, EMBED), F32),
                pltpu.VMEM((TILE_M, ROWS), F32), pltpu.VMEM((TILE_M, ROWS), F32),
                pltpu.VMEM((TILE_M, ROWS), BF16), pltpu.VMEM((TILE_M, ROWS), BF16),
                pltpu.VMEM((4, CHUNK_R, ROWS), F32),
                dma((2, 3, 9)), dma((2, 3, 9)), dma((9,)), dma((9,)), dma((3,)), dma((3,)), dma((2,)), dma((2,)),
                dma((4,)),
            ],
            compiler_params=pltpu.CompilerParams(
                collective_id=0, has_side_effects=True, vmem_limit_bytes=66_000_000),
            cost_estimate=pl.CostEstimate(flops=110_000_000_000, bytes_accessed=16_000_000, transcendentals=0),
        )(jnp.stack([temp_scale, logit_bias]), emb_img, emb_txt, pair_ids.reshape(1, ROWS),
          jnp.broadcast_to(pair_ids[:, None], (ROWS, 128)))
        grad_img = temp_scale * (part_img / total_rows)
        grad_txt = temp_scale * (part_txt / total_rows)
        dw_img = weight_grad(feat_img, unit_img, inv_img, grad_img)
        dw_txt = weight_grad(feat_txt, unit_txt, inv_txt, grad_txt)
        loss_sum = jnp.sum(sums[0]) + jnp.sum(sums[1])
        totals = lax.psum((loss_sum, jnp.sum(sums[2]), jnp.sum(sums[3]), dw_img, dw_txt), "data")
        return totals[0] / total_rows, temp_scale * (totals[1] / total_rows), totals[2] / total_rows, totals[3], totals[4]

    return jax.shard_map(
        local_fn,
        mesh=mesh,
        in_specs=(P("data", None), P("data", None), P(None, None), P(None, None), P(), P(), P("data")),
        out_specs=(P(), P(), P(), P(None, None), P(None, None)),
        check_vma=False,
    )
```

time: 1280 us -> 346 us (0.27)
  waiting for transfers between devices: 595 us -> 46 us
  matrix products: 353 us -> 17.7 us
  Pallas kernels: 0 us -> 203 us
  starting transfers between devices: 158 us -> 0.04 us
  local copies, waits for them, and re-layouts: 52.9 us -> 15.8 us
  blocking collectives: 61.1 us -> 30.5 us
  loops' own time: 27.1 us -> 0 us
    ppermute x46 -> x0, waiting for transfers between devices: 548 us -> none  [the longest x45 526 us: visit_block(): lax.ppermute((txt_blk, ids_blk, acc_txt + part_txt), 'data', next_perm)]
    dot_general x52 -> x4, matrix products: 353 us -> 17.7 us  [the longest x2 10.9 us: embed_rows(): raw_emb = jnp.dot(feat_rows, weights, preferred_element_type=F32)]
    pallas_call x0 -> x1, Pallas kernels: none -> 203 us  [local_fn(): pl.pallas_call(pair_kernel, out_shape=[jax.ShapeDtypeStruct((ROWS, EMBED)...]
    ppermute x46 -> x0, starting transfers between devices: 158 us -> none  [the longest x45 156 us: visit_block(): lax.ppermute((txt_blk, ids_blk, acc_txt + part_txt), 'data', next_perm)]
    while x92 -> x0, local copies, waits for them, and re-layouts: 36.9 us -> none
    psum x1, blocking collectives: 61.1 us -> 30.5 us  [local_fn(): lax.psum((loss_sum, jnp.sum(sums[2]), jnp.sum(sums[3]), dw_img, dw_txt),...]
    another operation x1 -> x0, loops' own time: 27.1 us -> none  [local_fn(): loop_state = lax.fori_loop(0, n_dev - 1, visit_block, loop_state)]
  transfers between devices with their start and end apart: 47 -> 1, of which waited for: 17 -> 1; matrix products, arithmetic and copies ran while one was open for 8% -> 0% of each run, Pallas kernels for 0% -> 0%
where the time goes in v1:
time: 346 us; the launch traced here: 344 us
  Pallas kernels  203 us (59%)
  waiting for transfers between devices  46 us (13%)
  blocking collectives  30.5 us (9%)
  between operations  21.9 us (6%)
  matrix products  17.7 us (5%)
  local copies, waits for them, and re-layouts  15.8 us (5%)
  other arithmetic  9.67 us (3%)
    pallas_call x1, Pallas kernels, local_fn(): pl.pallas_call(pair_kernel, out_shape=[jax.ShapeDtypeStruct((ROWS, EMBED)...  203 us
    psum x1, waiting for transfers between devices, local_fn(): lax.psum((loss_sum, jnp.sum(sums[2]), jnp.sum(sums[3]), dw_img, dw_txt),...  46 us
    psum x1, blocking collectives, local_fn(): lax.psum((loss_sum, jnp.sum(sums[2]), jnp.sum(sums[3]), dw_img, dw_txt),...  30.5 us
    dot_general x2, matrix products, embed_rows(): raw_emb = jnp.dot(feat_rows, weights, preferred_element_type=F32)  10.9 us
    unnamed x24, local copies, waits for them, and re-layouts  8.88 us
  transfers between devices with their start and end apart: 1, of which 1 were waited for; matrix products, arithmetic and copies ran while one was open for 0% of the time, Pallas kernels for 0%

profile of v1, /device:TPU:1, one launch (start us, length us, event | category | flops | bytes accessed | tf_op | source)
XLA Modules:
  0.0 344.4 jit_solution(12455995399511228468)
XLA Ops:
  7.2 0.0 all-reduce.4.cloned.1.call-start
  7.2 4.9 %multiply_reduce_fusion.2 = (f32[1024]{0:T(1024)S(1)}, f32[1024,768]{0,1:T(8,128)}) fusion(bf16[1024,768]{1,0:T(8,128)(2,1)} %param.8, bf16[768,768]{1,0:T(8,128)(2,1)} %param.10), kind=kOutput, calls=%fused_computation.4 | convolution fusion | flops 1209531392 | bytes 5902336 | tf_op jit(solution)/shard_map/dot_general | solution.py:22
  12.1 2.4 copy.13
  14.5 6.0 %multiply_reduce_fusion.3 = (f32[1024]{0:T(1024)S(1)}, f32[1024,768]{0,1:T(8,128)}) fusion(bf16[1024,768]{1,0:T(8,128)(2,1)} %param.7, bf16[768,768]{1,0:T(8,128)(2,1)} %param.9), kind=kOutput, calls=%fused_computation.5 | convolution fusion | flops 1209531392 | bytes 5902336 | tf_op jit(solution)/shard_map/dot_general | solution.py:22
  20.5 3.5 %copy.12 = f32[1024,768]{1,0:T(8,128)} copy(f32[1024,768]{0,1:T(8,128)} %get-tuple-element.26) | data formatting | bytes 6291456 | tf_op jit(solution)/shard_map/dot_general | solution.py:22
  25.4 1.4 multiply_convert_fusion.2.txt_ref
  26.8 1.1 copy-done.2
  27.8 1.4 multiply_convert_fusion.3.img_ref
  29.2 0.6 pad_maximum_fusion.scal_ref
  29.8 1.0 broadcast_in_dim.2.idrow_ref
  30.8 202.8 %shard_map.110 = (f32[1024,768]{1,0:T(8,128)}, f32[1024,768]{1,0:T(8,128)}, f32[4,16,1024]{2,1,0:T(8,128)}) custom-call(f32[2]{0:T(128)} %pad_maximum_fusion.scal_ref, bf16[1024,768]{1,0:T(8,128)(2,1)} %multiply_convert_fusion.3.img_ref, bf16[1024,768]{1,0:T(8,128)(2,1)} %multiply_convert_fusion.2.txt_ref, s32[1,1024]{1,0:T(1,128)} %bitcast.14, ...), custom_call_target="tpu_custom_call" | custom-call | flops 109999996928 | bytes 16000000 | tf_op jit(solution)/shard_map/pallas_call | solution.py:257
  233.7 5.6 %multiply_reduce_fusion = (f32[1024]{0:T(1024)S(1)}, f32[1024]{0:T(1024)S(1)}) fusion(f32[1024,768]{1,0:T(8,128)} %get-tuple-element.10, f32[1024,768]{1,0:T(8,128)} %copy-done, f32[]{:T(128)S(6)} %mul.78, f32[1024]{0:T(1024)S(1)} %rsqrt.17, f32[1024,768]{1,0:T(8,128)} %get-tuple-element.9, f32[1024,768]{1,0:T(8,128)} %copy.12, f32[1024]{0:T(1024)S(1)} %rsqrt.16), kind=kLoop, calls=%fused_computation.1 | loop fusion | flops 6289408 | bytes 12599300 | tf_op jit(solution)/shard_map/reduce_sum | solution.py:29
  239.3 0.8 copy-done.5
  240.2 0.4 copy-done.7
  240.6 3.4 convolution_bitcast_fusion
  244.0 0.5 copy-done.8
  244.5 3.4 convolution_bitcast_fusion.1
  247.9 0.0 all-reduce.4.cloned.1.call-update
  247.9 0.9 copy-done.9
  248.9 0.7 slice_reduce_fusion
  250.7 30.5 %all-reduce = (f32[]{:T(128)}, f32[]{:T(128)}, f32[]{:T(128)}) all-reduce(f32[]{:T(128)S(6)} %add.13, f32[]{:T(128)} %get-tuple-element.17, f32[]{:T(128)} %get-tuple-element.16), channel_id=1, replica_groups=mesh['data'=16] {'data'}, use_global_device_ids=true, to_apply=%region_4.0 | all-reduce | flops 3 | bytes 24 | tf_op jit(solution)/shard_map/psum | solution.py:284
  283.0 46.0 %all-reduce.4.cloned.1.call-done = (f32[768,768]{0,1:T(8,128)}, f32[768,768]{0,1:T(8,128)}) async-done(((f32[768,768]{0,1:T(8,128)}, f32[768,768]{0,1:T(8,128)}), (f32[768,768]{0,1:T(8,128)}, f32[768,768]{0,1:T(8,128)})) %all-reduce.4.cloned.1.call-update) | async-done | bytes 4718608 | tf_op jit(solution)/shard_map/psum | solution.py:284
  329.0 3.2 copy.14
  332.2 1.9 copy.15
  (19 shorter events, 0.0 us)
Async XLA Ops:
  7.2 321.8 %all-reduce.4.cloned.1.call-start = ((), (), s32[]{:S(2)}) async-start(), calls=%async_computation | async-start | bytes 9437184 | tf_op jit(solution)/shard_map/psum | solution.py:284
  14.4 10.9 %copy-start = (f32[1024,768]{1,0:T(8,128)}, f32[1024,768]{1,0:T(8,128)S(1)}, u32[]{:S(2)}) copy-start(f32[1024,768]{1,0:T(8,128)S(1)} %copy.13) | copy-start | bytes 9437188
  25.4 2.5 copy-start.2
  27.8 2.0 copy-start.10
  233.6 5.7 %copy-start.1 = (f32[1024,768]{1,0:T(8,128)S(1)}, f32[1024,768]{1,0:T(8,128)}, u32[]{:S(2)}) copy-start(f32[1024,768]{1,0:T(8,128)} %copy-done) | copy-start | bytes 9437188
  233.7 6.5 %copy-start.5 = (f32[1024,768]{1,0:T(8,128)S(1)}, f32[1024,768]{1,0:T(8,128)}, u32[]{:S(2)}) copy-start(f32[1024,768]{1,0:T(8,128)} %get-tuple-element.10) | copy-start | bytes 9437188
  233.7 6.9 %copy-start.7 = (bf16[1024,768]{1,0:T(8,128)(2,1)S(1)}, bf16[1024,768]{1,0:T(8,128)(2,1)}, u32[]{:S(2)}) copy-start(bf16[1024,768]{1,0:T(8,128)(2,1)} %param.8) | copy-start | bytes 4718596
  240.6 3.4 copy-start.3
  240.6 3.4 copy-start.4
  240.6 3.9 %copy-start.8 = (bf16[1024,768]{1,0:T(8,128)(2,1)S(1)}, bf16[1024,768]{1,0:T(8,128)(2,1)}, u32[]{:S(2)}) copy-start(bf16[1024,768]{1,0:T(8,128)(2,1)} %param.7) | copy-start | bytes 4718596
  247.9 0.9 copy-start.9
  329.0 3.2 copy-start.6
Sparse Core Ops, SparseCore 0:
  248.1 80.9 all-reduce.3

commit v2 on v1

--- a/solution.py
+++ b/solution.py
@@ -16,18 +16,6 @@
 SLOT = {0: 0, 1: 2, 2: 3, 4: 4, 3: 5, 6: 6, 5: 7, 7: 8}
 PART_ROWS = ((0, 352), (352, 336), (688, 336))
 PART_DIMS = ((1, 2, 4), (2, 4, 1), (4, 1, 2))
-
-
-def embed_rows(feat_rows, weights):
-    raw_emb = jnp.dot(feat_rows, weights, preferred_element_type=F32)
-    inv_norm = lax.rsqrt(jnp.sum(raw_emb * raw_emb, axis=1, keepdims=True))
-    unit_emb = raw_emb * inv_norm
-    return unit_emb, inv_norm, unit_emb.astype(BF16)
-
-
-def weight_grad(feat_rows, unit_emb, inv_norm, grad_emb):
-    raw_grad = inv_norm * (grad_emb - unit_emb * jnp.sum(unit_emb * grad_emb, axis=1, keepdims=True))
-    return lax.dot_general(feat_rows, raw_grad.astype(BF16), CONTRACT_ROWS, preferred_element_type=F32)
 
 
 def gather_plan():
@@ -44,7 +32,7 @@
     return own, first, last
 
 
-def pair_kernel(scal_ref, img_ref, txt_ref, ids_ref, idrow_ref, dimg_ref, dtxt_ref, sums_ref,
+def pair_kernel(scal_ref, feat_img, feat_txt, w_img, w_txt, ids_ref, idrow_ref, dimg_ref, dtxt_ref, sums_ref,
                 slots, ids_all, id_rows, acc, partner, s0, s1, g0, g1, sums,
                 send_sem, recv_sem, ids_send, ids_recv, pair_send, pair_recv, grad_send, grad_recv, load_sem):
     me = lax.axis_index("data")
@@ -59,20 +47,30 @@
         return where * 2 + core
 
     other_core = chip * 2 + (1 - core)
-    loads = [pltpu.make_async_copy(src, slots.at[a, 0], load_sem.at[a]) for a, src in ((0, txt_ref), (1, img_ref))]
+    loads = [pltpu.make_async_copy(src, slots.at[a, 8], load_sem.at[2 * a]) for a, src in ((0, feat_txt), (1, feat_img))]
+    loads += [pltpu.make_async_copy(src, slots.at[a, 7, pl.ds(0, EMBED)], load_sem.at[2 * a + 1])
+              for a, src in ((0, w_txt), (1, w_img))]
+    loads.append(pltpu.make_async_copy(ids_ref, ids_all.at[0], load_sem.at[4]))
+    loads.append(pltpu.make_async_copy(idrow_ref, id_rows.at[pl.ds(0, ROWS)], load_sem.at[5]))
     for c in loads:
         c.start()
-    id_load = pltpu.make_async_copy(ids_ref, ids_all.at[0], load_sem.at[2])
-    id_load.start()
-    loads.append(pltpu.make_async_copy(idrow_ref, id_rows.at[pl.ds(0, ROWS)], load_sem.at[3]))
-    loads[2].start()
+    acc[...] = jnp.zeros_like(acc)
+    sums[...] = jnp.zeros_like(sums)
+    for c in loads:
+        c.wait()
+
+    def embed(i, carry):
+        a, rows = i // 2, pl.ds(pl.multiple_of((i % 2) * (ROWS // 2), ROWS // 2), ROWS // 2)
+        raw = jnp.dot(slots[a, 8, rows, :], slots[a, 7, 0:EMBED, :], preferred_element_type=F32)
+        slots[a, 0, rows, :] = (raw * lax.rsqrt(jnp.sum(raw * raw, axis=1, keepdims=True))).astype(BF16)
+        return carry
+
+    lax.fori_loop(0, 4, embed, 0)
 
     barrier = pltpu.get_barrier_semaphore()
     partners = [other_core] + [peer(rel) for rel in range(1, 8)]
     for dev in partners:
         pl.semaphore_signal(barrier, inc=1, device_id=(dev,), device_id_type=MESH)
-    acc[...] = jnp.zeros_like(acc)
-    sums[...] = jnp.zeros_like(sums)
     pl.semaphore_wait(barrier, len(partners))
 
     def part_copy(a, p, rel, d):
@@ -101,11 +99,8 @@
         id_copies.append(pltpu.make_async_remote_copy(
             src_ref=ids_all.at[0], dst_ref=ids_all.at[rel_slot], send_sem=ids_send.at[rel_slot],
             recv_sem=ids_recv.at[rel_slot], device_id=(dev,), device_id_type=MESH))
-    id_load.wait()
     for c in id_copies:
         c.start()
-    for c in loads:
-        c.wait()
     for c in pair_copies[::-1]:
         c.start()
     for send in own:
@@ -230,7 +225,9 @@
     acc[1, 0:ROWS, :] += partner[1]
     outs = [pltpu.make_async_copy(acc.at[x, pl.ds(0, ROWS)], ref, load_sem.at[x]) for x, ref in ((1, dimg_ref), (0, dtxt_ref))]
     outs[0].start()
-    sums_ref[...] = sums[...]
+    for x in range(4):
+        rows = sums[x, 0:8, :] + sums[x, 8:16, :]
+        sums_ref[x] = sum(rows[:, v:v + 128] for v in range(0, ROWS, 128))
     grad_copies[0].wait_recv()
     acc[0, 0:ROWS, :] += partner[0]
     outs[1].start()
@@ -243,21 +240,148 @@
             part_copy(a, *send).wait_send()
 
 
+def tail_kernel(scal_ref, feat_img, feat_txt, w_img, w_txt, part_img, part_txt, sums_ref, dw_img_ref, dw_txt_ref, tot_ref,
+                feats, heads, parts, raw_grad, mine, full, from_core, landing, stats,
+                load_sem, core_send, core_recv, rs_send, rs_recv, ag_send, ag_recv, out_send, out_recv, st_send, st_recv, ready):
+    me = lax.axis_index("data")
+    core, chip = me % 2, me // 2
+    other_core = chip * 2 + (1 - core)
+    near = {d: (chip + d * (1 - 2 * ((chip // d) % 2))) * 2 + core for d in (1, 2, 4)}
+    others = [(me + k) % 16 for k in range(1, 16)]
+
+    loads = []
+    for a, refs in enumerate(((feat_img, w_img, part_img), (feat_txt, w_txt, part_txt))):
+        loads += [pltpu.make_async_copy(src, dst.at[a], load_sem.at[a, k])
+                  for k, (src, dst) in enumerate(zip(refs, (feats, heads, parts)))]
+    for c in loads:
+        c.start()
+    barrier = pltpu.get_barrier_semaphore()
+    for dev in others:
+        pl.semaphore_signal(barrier, inc=1, device_id=(dev,), device_id_type=MESH)
+    for c in loads:
+        c.wait()
+    scale = scal_ref[0]
+    total_rows = 16 * ROWS
+
+    def head_grad(a, dst):
+        def rows_step(i, carry):
+            rows = pl.ds(pl.multiple_of(i * 256, 256), 256)
+            raw = jnp.dot(feats[a, rows, :], heads[a], preferred_element_type=F32)
+            inv = lax.rsqrt(jnp.sum(raw * raw, axis=1, keepdims=True))
+            unit = raw * inv
+            grad = scale * (parts[a, rows, :] * F32(1.0 / total_rows))
+            raw_grad[rows, :] = (inv * (grad - unit * jnp.sum(unit * grad, axis=1, keepdims=True))).astype(BF16)
+            return carry
+
+        lax.fori_loop(0, ROWS // 256, rows_step, 0)
+        dst[...] = lax.dot_general(feats[a], raw_grad[...], CONTRACT_ROWS, preferred_element_type=F32)
+
+    head_grad(1 - core, full.at[1 - core])
+    pl.semaphore_wait(barrier, len(others))
+    to_core = pltpu.make_async_remote_copy(
+        src_ref=full.at[1 - core], dst_ref=from_core, send_sem=core_send, recv_sem=core_recv,
+        device_id=(other_core,), device_id_type=MESH)
+    to_core.start()
+    stats[me] = sums_ref[...]
+    stat_copies = [pltpu.make_async_remote_copy(
+        src_ref=stats.at[me], dst_ref=stats.at[me], send_sem=st_send.at[k], recv_sem=st_recv.at[k],
+        device_id=(dev,), device_id_type=MESH) for k, dev in enumerate(others)]
+    for c in stat_copies:
+        c.start()
+    head_grad(core, mine)
+    to_core.wait_recv()
+    mine[...] += from_core[...]
+
+    lows = [256 * p for p in range(3)]
+    kept = []
+    sent = []
+    for k, half in enumerate((128, 64, 32)):
+        base = (0, 128, 192)[k]
+        copies = []
+        for p in range(3):
+            d = PART_DIMS[p][k]
+            bit = (chip // d) % 2
+            src = pl.multiple_of(lows[p] + (1 - bit) * half, 32)
+            copies.append(pltpu.make_async_remote_copy(
+                src_ref=mine.at[pl.ds(src, half)], dst_ref=landing.at[p, pl.ds(base, half)],
+                send_sem=rs_send.at[k, p], recv_sem=rs_recv.at[k, p], device_id=(near[d],), device_id_type=MESH))
+            copies[-1].start()
+        kept.append(list(lows))
+        for p in range(3):
+            bit = (chip // PART_DIMS[p][k]) % 2
+            lows[p] = lows[p] + bit * half
+            copies[p].wait_recv()
+            rows = pl.ds(pl.multiple_of(lows[p], 32), half)
+            total = mine[rows, :] + landing[p, base:base + half, :]
+            if k < 2:
+                mine[rows, :] = total
+            else:
+                full[core, rows, :] = total
+        sent += copies
+
+    def share(low, size, p, k):
+        rows = pl.ds(pl.multiple_of(low, 32), size)
+        return pltpu.make_async_remote_copy(
+            src_ref=full.at[core, rows], dst_ref=full.at[core, rows], send_sem=out_send.at[p, k],
+            recv_sem=out_recv.at[p, k], device_id=(other_core,), device_id_type=MESH)
+
+    to_core.wait_send()
+    pl.semaphore_signal(ready, inc=1, device_id=(other_core,), device_id_type=MESH)
+    pl.semaphore_wait(ready, 1)
+    shares = []
+    for k in (2, 1, 0):
+        size = (128, 64, 32)[k]
+        copies = []
+        for p in range(3):
+            d = PART_DIMS[p][k]
+            rows = pl.ds(pl.multiple_of(lows[p], 32), size)
+            copies.append(pltpu.make_async_remote_copy(
+                src_ref=full.at[core, rows], dst_ref=full.at[core, rows], send_sem=ag_send.at[k, p],
+                recv_sem=ag_recv.at[k, p], device_id=(near[d],), device_id_type=MESH))
+            copies[-1].start()
+        if k == 2:
+            for p in range(3):
+                shares.append(share(lows[p], size, p, 3))
+                shares[-1].start()
+        for p in range(3):
+            bit = (chip // PART_DIMS[p][k]) % 2
+            copies[p].wait_recv()
+            shares.append(share(kept[k][p] + (1 - bit) * size, size, p, k))
+            shares[-1].start()
+            lows[p] = kept[k][p]
+        sent += copies
+    write_mine = [pltpu.make_async_copy(full.at[a], ref, load_sem.at[a, 0]) for a, ref in ((0, dw_img_ref), (1, dw_txt_ref))]
+    for c in stat_copies:
+        c.wait_recv()
+    total = stats[0]
+    for dev in range(1, 16):
+        total = total + stats[dev]
+    tot_ref[...] = jnp.broadcast_to(jnp.sum(jnp.sum(total, axis=1, keepdims=True), axis=2, keepdims=True), (4, 8, 128))
+    for c in shares:
+        c.wait_recv()
+    for c in write_mine:
+        c.start()
+    for c in sent + shares + stat_copies:
+        c.wait_send()
+    for c in write_mine:
+        c.wait()
+
+
 def solution(mesh):
     n_dev = mesh.shape["data"]
 
     def local_fn(feat_img, feat_txt, w_img, w_txt, log_temp, logit_bias, pair_ids):
         total_rows = feat_img.shape[0] * n_dev
         temp_scale = jnp.exp(log_temp)
-        unit_img, inv_img, emb_img = embed_rows(feat_img, w_img)
-        unit_txt, inv_txt, emb_txt = embed_rows(feat_txt, w_txt)
+        scal = jnp.stack([temp_scale, logit_bias])
         vmem = pl.BlockSpec(memory_space=pltpu.VMEM)
+        smem = pl.BlockSpec(memory_space=pltpu.SMEM)
         hbm = pl.BlockSpec(memory_space=pl.ANY)
         dma = pltpu.SemaphoreType.DMA
         part_img, part_txt, sums = pl.pallas_call(
             pair_kernel,
-            out_shape=[jax.ShapeDtypeStruct((ROWS, EMBED), F32)] * 2 + [jax.ShapeDtypeStruct((4, CHUNK_R, ROWS), F32)],
-            in_specs=[pl.BlockSpec(memory_space=pltpu.SMEM), hbm, hbm, hbm, hbm],
+            out_shape=[jax.ShapeDtypeStruct((ROWS, EMBED), F32)] * 2 + [jax.ShapeDtypeStruct((4, 8, 128), F32)],
+            in_specs=[smem] + [hbm] * 6,
             out_specs=[hbm, hbm, vmem],
             scratch_shapes=[
                 pltpu.VMEM((2, 9, ROWS, EMBED), BF16),
@@ -269,20 +393,32 @@
                 pltpu.VMEM((TILE_M, ROWS), BF16), pltpu.VMEM((TILE_M, ROWS), BF16),
                 pltpu.VMEM((4, CHUNK_R, ROWS), F32),
                 dma((2, 3, 9)), dma((2, 3, 9)), dma((9,)), dma((9,)), dma((3,)), dma((3,)), dma((2,)), dma((2,)),
-                dma((4,)),
+                dma((6,)),
             ],
             compiler_params=pltpu.CompilerParams(
                 collective_id=0, has_side_effects=True, vmem_limit_bytes=66_000_000),
             cost_estimate=pl.CostEstimate(flops=110_000_000_000, bytes_accessed=16_000_000, transcendentals=0),
-        )(jnp.stack([temp_scale, logit_bias]), emb_img, emb_txt, pair_ids.reshape(1, ROWS),
+        )(scal, feat_img, feat_txt, w_img, w_txt, pair_ids.reshape(1, ROWS),
           jnp.broadcast_to(pair_ids[:, None], (ROWS, 128)))
-        grad_img = temp_scale * (part_img / total_rows)
-        grad_txt = temp_scale * (part_txt / total_rows)
-        dw_img = weight_grad(feat_img, unit_img, inv_img, grad_img)
-        dw_txt = weight_grad(feat_txt, unit_txt, inv_txt, grad_txt)
-        loss_sum = jnp.sum(sums[0]) + jnp.sum(sums[1])
-        totals = lax.psum((loss_sum, jnp.sum(sums[2]), jnp.sum(sums[3]), dw_img, dw_txt), "data")
-        return totals[0] / total_rows, temp_scale * (totals[1] / total_rows), totals[2] / total_rows, totals[3], totals[4]
+        dw_img, dw_txt, totals = pl.pallas_call(
+            tail_kernel,
+            out_shape=[jax.ShapeDtypeStruct((EMBED, EMBED), F32)] * 2 + [jax.ShapeDtypeStruct((4, 8, 128), F32)],
+            in_specs=[smem] + [hbm] * 6 + [vmem],
+            out_specs=[hbm, hbm, vmem],
+            scratch_shapes=[
+                pltpu.VMEM((2, ROWS, EMBED), BF16), pltpu.VMEM((2, EMBED, EMBED), BF16),
+                pltpu.VMEM((2, ROWS, EMBED), F32), pltpu.VMEM((ROWS, EMBED), BF16),
+                pltpu.VMEM((EMBED, EMBED), F32), pltpu.VMEM((2, EMBED, EMBED), F32), pltpu.VMEM((EMBED, EMBED), F32),
+                pltpu.VMEM((3, 224, EMBED), F32), pltpu.VMEM((16, 4, 8, 128), F32),
+                dma((2, 3)), dma, dma, dma((3, 3)), dma((3, 3)), dma((3, 3)), dma((3, 3)), dma((3, 4)), dma((3, 4)),
+                dma((15,)), dma((15,)), pltpu.SemaphoreType.REGULAR,
+            ],
+            compiler_params=pltpu.CompilerParams(
+                collective_id=1, has_side_effects=True, vmem_limit_bytes=60_000_000),
+            cost_estimate=pl.CostEstimate(flops=5_000_000_000, bytes_accessed=16_000_000, transcendentals=0),
+        )(scal, feat_img, feat_txt, w_img, w_txt, part_img, part_txt, sums)
+        loss_sum, temp_sum, bias_sum = totals[0, 0, 0] + totals[1, 0, 0], totals[2, 0, 0], totals[3, 0, 0]
+        return loss_sum / total_rows, temp_scale * (temp_sum / total_rows), bias_sum / total_rows, dw_img, dw_txt
 
     return jax.shard_map(
         local_fn,

time: 346 us -> 286 us (0.83)
  Pallas kernels: 203 us -> 269 us
  waiting for transfers between devices: 46 us -> 0 us
  blocking collectives: 30.5 us -> 0 us
  matrix products: 17.7 us -> 0 us
  between operations: 21.9 us -> 7.98 us
  other arithmetic: 9.67 us -> 0.59 us
  local copies, waits for them, and re-layouts: 15.8 us -> 7.68 us
    pallas_call x0 -> x1, Pallas kernels: none -> 60.4 us  [local_fn(): pl.pallas_call(tail_kernel, out_shape=[jax.ShapeDtypeStruct((EMBED, EMBED...]
    psum x1 -> x0, waiting for transfers between devices: 46 us -> none  [local_fn(): lax.psum((loss_sum, jnp.sum(sums[2]), jnp.sum(sums[3]), dw_img, dw_txt),...]
    psum x1 -> x0, blocking collectives: 30.5 us -> none  [local_fn(): lax.psum((loss_sum, jnp.sum(sums[2]), jnp.sum(sums[3]), dw_img, dw_txt),...]
    dot_general x4 -> x0, matrix products: 17.7 us -> none  [the longest x2 10.9 us: embed_rows(): raw_emb = jnp.dot(feat_rows, weights, preferred_element_type=F32)]
    reduce_sum x2 -> x0, other arithmetic: 6.32 us -> none  [the longest x1 5.63 us: weight_grad(): jnp.sum(unit_emb * grad_emb, axis=1, keepdims=True)]
    pallas_call x1, Pallas kernels: 203 us -> 209 us  [local_fn(): pl.pallas_call(pair_kernel, out_shape=[jax.ShapeDtypeStruct((ROWS, EMBED)...]
    dot_general x2 -> x0, local copies, waits for them, and re-layouts: 5.92 us -> none  [embed_rows(): raw_emb = jnp.dot(feat_rows, weights, preferred_element_type=F32)]
    unnamed x24 -> x4, local copies, waits for them, and re-layouts: 8.88 us -> 4.78 us
  transfers between devices with their start and end apart: 1 -> 0, of which waited for: 1 -> 0; matrix products, arithmetic and copies ran while one was open for 0% -> 0% of each run, Pallas kernels for 0% -> 0%
where the time goes in v2:
time: 286 us
  Pallas kernels  269 us (94%)
  between operations  7.98 us (3%)
  local copies, waits for them, and re-layouts  7.68 us (3%)
    pallas_call x1, Pallas kernels, local_fn(): pl.pallas_call(pair_kernel, out_shape=[jax.ShapeDtypeStruct((ROWS, EMBED)...  209 us
    pallas_call x1, Pallas kernels, local_fn(): pl.pallas_call(tail_kernel, out_shape=[jax.ShapeDtypeStruct((EMBED, EMBED...  60.4 us

profile of v2, /device:TPU:1, one launch (start us, length us, event | category | flops | bytes accessed | tf_op | source)
XLA Modules:
  0.0 285.6 jit_solution(15659180506984841209)
XLA Ops:
  2.0 0.6 pad_maximum_fusion.scal_ref
  2.5 1.7 broadcast_in_dim.2.idrow_ref
  4.2 209.0 %shard_map.110 = (f32[1024,768]{1,0:T(8,128)}, f32[1024,768]{1,0:T(8,128)}, f32[4,8,128]{2,1,0:T(8,128)}) custom-call(f32[2]{0:T(128)} %pad_maximum_fusion.scal_ref, bf16[1024,768]{1,0:T(8,128)(2,1)} %feat_img.3, bf16[1024,768]{1,0:T(8,128)(2,1)} %feat_txt.3, bf16[768,768]{1,0:T(8,128)(2,1)} %w_img.3, bf16[768,768]{1,0:T(8,128)(2,1)} %w_txt.3, ...), custom_call_target="tpu_custom_call" | custom-call | flops 109999996928 | bytes 16000000 | tf_op jit(solution)/shard_map/pallas_call | solution.py:381
  213.2 60.4 %shard_map.111 = (f32[768,768]{1,0:T(8,128)}, f32[768,768]{1,0:T(8,128)}, f32[4,8,128]{2,1,0:T(8,128)}) custom-call(f32[2]{0:T(128)} %pad_maximum_fusion.scal_ref, bf16[1024,768]{1,0:T(8,128)(2,1)} %feat_img.3, bf16[1024,768]{1,0:T(8,128)(2,1)} %feat_txt.3, bf16[768,768]{1,0:T(8,128)(2,1)} %w_img.3, bf16[768,768]{1,0:T(8,128)(2,1)} %w_txt.3, ...), custom_call_target="tpu_custom_call" | custom-call | flops 5000000000 | bytes 16000000 | tf_op jit(solution)/shard_map/pallas_call | solution.py:403
  273.6 1.2 fusion
  277.5 0.0 copy-start
  277.5 3.4 %copy.16 = f32[768,768]{1,0:T(8,128)} copy(f32[768,768]{1,0:T(8,128)} %get-tuple-element.29) | data formatting | bytes 4718592
  280.8 0.0 copy-done
  280.8 1.4 copy.17
Async XLA Ops:
  277.5 3.4 %copy-start = (f32[768,768]{1,0:T(8,128)S(1)}, f32[768,768]{1,0:T(8,128)}, u32[]{:S(2)}) copy-start(f32[768,768]{1,0:T(8,128)} %get-tuple-element.30) | copy-start | bytes 7077892

commit v3 on v2

--- a/solution.py
+++ b/solution.py
@@ -13,27 +13,27 @@
 CONTRACT_ROWS = (((0,), (0,)), ((), ()))
 CONTRACT_COLS = (((1,), (1,)), ((), ()))
 
-SLOT = {0: 0, 1: 2, 2: 3, 4: 4, 3: 5, 6: 6, 5: 7, 7: 8}
 PART_ROWS = ((0, 352), (352, 336), (688, 336))
 PART_DIMS = ((1, 2, 4), (2, 4, 1), (4, 1, 2))
 
 
-def gather_plan():
-    own = [(p, 0, PART_DIMS[p][k]) for k in range(3) for p in range(3)]
-    first, last = [], []
-    for p, (d1, d2, d3) in enumerate(PART_DIMS):
-        first.append((p, d1, d2))
-    for p, (d1, d2, d3) in enumerate(PART_DIMS):
-        first.append((p, d1, d3))
-    for p, (d1, d2, d3) in enumerate(PART_DIMS):
-        first.append((p, d2, d3))
-    for p, (d1, d2, d3) in enumerate(PART_DIMS):
-        last.append((p, d1 | d2, d3))
-    return own, first, last
+def turn_rel(turn, part):
+    dims = PART_DIMS[part]
+    return {0: dims[0], 1: dims[1], 2: dims[2], 3: dims[0] | dims[1], 4: dims[0] | dims[2], 5: dims[1] | dims[2],
+            6: 7}[turn]
+
+
+SLOT = {(part, turn_rel(turn, part)): 2 + turn for turn in range(7) for part in range(3)}
+SLOT.update({(part, 0): 0 for part in range(3)})
+
+
+def turn_sends(turn):
+    ways = {-1: ((None, 0), (None, 1), (None, 2)), 0: ((0, 1), (0, 2)), 1: ((1, 2),), 3: ((3, 2),)}.get(turn, ())
+    return [(p, 0 if turn < 0 else turn_rel(turn, p), PART_DIMS[p][k]) for _, k in ways for p in range(3)]
 
 
 def pair_kernel(scal_ref, feat_img, feat_txt, w_img, w_txt, ids_ref, idrow_ref, dimg_ref, dtxt_ref, sums_ref,
-                slots, ids_all, id_rows, acc, partner, s0, s1, g0, g1, sums,
+                slots, ids_raw, ids_all, id_rows, acc, partner, s0, s1, g0, g1, sums,
                 send_sem, recv_sem, ids_send, ids_recv, pair_send, pair_recv, grad_send, grad_recv, load_sem):
     me = lax.axis_index("data")
     core = me % 2
@@ -50,7 +50,7 @@
     loads = [pltpu.make_async_copy(src, slots.at[a, 8], load_sem.at[2 * a]) for a, src in ((0, feat_txt), (1, feat_img))]
     loads += [pltpu.make_async_copy(src, slots.at[a, 7, pl.ds(0, EMBED)], load_sem.at[2 * a + 1])
               for a, src in ((0, w_txt), (1, w_img))]
-    loads.append(pltpu.make_async_copy(ids_ref, ids_all.at[0], load_sem.at[4]))
+    loads.append(pltpu.make_async_copy(ids_ref, ids_raw.at[0], load_sem.at[4]))
     loads.append(pltpu.make_async_copy(idrow_ref, id_rows.at[pl.ds(0, ROWS)], load_sem.at[5]))
     for c in loads:
         c.start()
@@ -76,17 +76,16 @@
     def part_copy(a, p, rel, d):
         lo, size = PART_ROWS[p]
         return pltpu.make_async_remote_copy(
-            src_ref=slots.at[a, SLOT[rel], pl.ds(lo, size)],
-            dst_ref=slots.at[a, SLOT[rel ^ d], pl.ds(lo, size)],
-            send_sem=send_sem.at[a, p, SLOT[rel ^ d]],
-            recv_sem=recv_sem.at[a, p, SLOT[rel ^ d]],
+            src_ref=slots.at[a, SLOT[p, rel], pl.ds(lo, size)],
+            dst_ref=slots.at[a, SLOT[p, rel ^ d], pl.ds(lo, size)],
+            send_sem=send_sem.at[a, p, SLOT[p, rel ^ d]],
+            recv_sem=recv_sem.at[a, p, SLOT[p, rel ^ d]],
             device_id=(peer(d),), device_id_type=MESH)
 
     def arrival(a, p, rel):
         d = next(x for x in reversed(PART_DIMS[p]) if rel & x)
         part_copy(a, p, rel ^ d, d).wait_recv()
 
-    own, first, last = gather_plan()
     pair_copies = [pltpu.make_async_remote_copy(
         src_ref=slots.at[a, 0], dst_ref=slots.at[a, 1], send_sem=pair_send.at[a], recv_sem=pair_recv.at[a],
         device_id=(other_core,), device_id_type=MESH) for a in range(2)]
@@ -95,20 +94,26 @@
         recv_sem=pair_recv.at[2], device_id=(other_core,), device_id_type=MESH))
     id_copies = []
     for i, dev in enumerate(partners):
-        rel_slot = 1 if i == 0 else SLOT[i]
-        id_copies.append(pltpu.make_async_remote_copy(
-            src_ref=ids_all.at[0], dst_ref=ids_all.at[rel_slot], send_sem=ids_send.at[rel_slot],
-            recv_sem=ids_recv.at[rel_slot], device_id=(dev,), device_id_type=MESH))
+        if i > 0:
+            id_copies.append(pltpu.make_async_remote_copy(
+                src_ref=ids_raw.at[0], dst_ref=ids_raw.at[i], send_sem=ids_send.at[i],
+                recv_sem=ids_recv.at[i], device_id=(dev,), device_id_type=MESH))
     for c in id_copies:
         c.start()
     for c in pair_copies[::-1]:
         c.start()
-    for send in own:
+    for send in turn_sends(-1):
         part_copy(0, *send).start()
 
     scale, bias = scal_ref[0], scal_ref[1]
     for c in id_copies:
         c.wait_recv()
+    lane = lax.broadcasted_iota(jnp.int32, (1, ROWS), 1)
+    ids_all[0] = ids_raw[0]
+    for turn in range(7):
+        ids_all[2 + turn] = jnp.where(
+            lane < PART_ROWS[1][0], ids_raw[turn_rel(turn, 0)],
+            jnp.where(lane < PART_ROWS[2][0], ids_raw[turn_rel(turn, 1)], ids_raw[turn_rel(turn, 2)]))
     for c in pair_copies:
         c.wait_recv()
 
@@ -117,13 +122,16 @@
     def slot_of(block):
         return block + (block + 7) // 8
 
+    def row_tile(t):
+        return (t % n_m + (n_m // 2) * ((t // n_m + 7) // 8)) % n_m
+
     def scores(a, t, s_ref):
-        m, slot = pl.multiple_of((t % n_m) * TILE_M, TILE_M), slot_of(t // n_m)
-        rows = slots[1 - a, (t % n_m) // (n_m // 2), pl.ds(pl.multiple_of((t % (n_m // 2)) * TILE_M, TILE_M), TILE_M), :]
+        m, slot = pl.multiple_of(row_tile(t) * TILE_M, TILE_M), slot_of(t // n_m)
+        rows = slots[1 - a, m // ROWS, pl.ds(pl.multiple_of(m % ROWS, TILE_M), TILE_M), :]
         s_ref[...] = lax.dot_general(rows, slots[a, slot], CONTRACT_COLS, preferred_element_type=F32)
 
     def tile_grad(a, t, s_ref, g_ref):
-        m, slot = pl.multiple_of((t % n_m) * TILE_M, TILE_M), slot_of(t // n_m)
+        m, slot = pl.multiple_of(row_tile(t) * TILE_M, TILE_M), slot_of(t // n_m)
 
         col_ids = ids_all[slot]
 
@@ -149,44 +157,21 @@
         sums[2 * a + 1] = sums[1] + jnp.log1p(x1) if a == 0 else x1
 
     def row_grad(a, t, g_ref):
-        m, slot = pl.multiple_of((t % n_m) * TILE_M, TILE_M), slot_of(t // n_m)
+        m, slot = pl.multiple_of(row_tile(t) * TILE_M, TILE_M), slot_of(t // n_m)
         acc[1 - a, pl.ds(m, TILE_M), :] += jnp.dot(g_ref[...], slots[a, slot], preferred_element_type=F32)
 
-    def block_needs(a, rel, seen):
-        return [(a, p, rel) for p in range(3) if (a, p, rel) not in seen]
-
-    order = sorted(SLOT, key=SLOT.get)
-    seen = set()
-    steps = {}
-
-    def add(key, waits=(), sends=()):
-        w = [x for x in dict.fromkeys(waits) if x not in seen]
-        seen.update(w)
-        steps.setdefault(key, []).append((w, list(sends)))
-
-    def forwards(a, sends):
-        return [(a, p, rel) for p, rel, _ in sends], [(a,) + s for s in sends]
-
-    add((0, 1), *forwards(0, first))
-    add((0, 1), block_needs(0, order[1], seen))
-    add((0, 2), block_needs(0, order[2], seen))
-    add((0, 2), *forwards(0, last))
-    add((0, 2), (), [(1,) + s for s in own])
-    for b in range(3, 8):
-        add((0, b), block_needs(0, order[b], seen))
-    add((0, 7), *forwards(1, first))
-    add((1, 1), block_needs(1, order[1], seen))
-    add((1, 2), block_needs(1, order[2], seen))
-    add((1, 2), *forwards(1, last))
-    for b in range(3, 8):
-        add((1, b), block_needs(1, order[b], seen))
-
-    def run_steps(key):
-        for waits, sends in steps.get(key, ()):
-            for w in waits:
-                arrival(*w)
-            for s in sends:
-                part_copy(*s).start()
+    def run_turn(a, turn):
+        for p in range(3):
+            arrival(a, p, turn_rel(turn, p))
+        for send in turn_sends(turn):
+            part_copy(a, *send).start()
+        if (a, turn) == (0, 3):
+            for send in turn_sends(-1):
+                part_copy(1, *send).start()
+
+    grad_copies = [pltpu.make_async_remote_copy(
+        src_ref=acc.at[x, pl.ds(ROWS, ROWS)], dst_ref=partner.at[x], send_sem=grad_send.at[x],
+        recv_sem=grad_recv.at[x], device_id=(other_core,), device_id_type=MESH) for x in range(2)]
 
     def stream(a):
         t0, t_end = 0, 8 * n_m
@@ -199,7 +184,7 @@
             for b in range(1, 8):
                 @pl.when(t + 1 == b * n_m)
                 def _():
-                    run_steps((a, b))
+                    run_turn(a, b - 1)
             scores(a, t + 1, s0)
             tile_grad(a, t, s1, g1)
             row_grad(a, t - 1, g0)
@@ -209,18 +194,13 @@
             return carry
 
         lax.fori_loop(0, (t_end - t0 - 2) // 2, body, 0)
+        grad_copies[1 - a].start()
         tile_grad(a, t_end - 1, s1, g1)
         row_grad(a, t_end - 2, g0)
         row_grad(a, t_end - 1, g1)
 
-    grad_copies = [pltpu.make_async_remote_copy(
-        src_ref=acc.at[x, pl.ds(ROWS, ROWS)], dst_ref=partner.at[x], send_sem=grad_send.at[x],
-        recv_sem=grad_recv.at[x], device_id=(other_core,), device_id_type=MESH) for x in range(2)]
-
     stream(0)
-    grad_copies[1].start()
     stream(1)
-    grad_copies[0].start()
     grad_copies[1].wait_recv()
     acc[1, 0:ROWS, :] += partner[1]
     outs = [pltpu.make_async_copy(acc.at[x, pl.ds(0, ROWS)], ref, load_sem.at[x]) for x, ref in ((1, dimg_ref), (0, dtxt_ref))]
@@ -236,7 +216,7 @@
     for c in grad_copies + pair_copies + id_copies:
         c.wait_send()
     for a in range(2):
-        for send in own + first + last:
+        for send in [x for turn in (-1, 0, 1, 3) for x in turn_sends(turn)]:
             part_copy(a, *send).wait_send()
 
 
@@ -292,64 +272,70 @@
     to_core.wait_recv()
     mine[...] += from_core[...]
 
-    lows = [256 * p for p in range(3)]
-    kept = []
+    bits = [[(chip // PART_DIMS[p][k]) % 2 for k in range(3)] for p in range(3)]
+    lows = [[256 * p] for p in range(3)]
+    for p in range(3):
+        for k, half in enumerate((128, 64, 32)):
+            lows[p].append(lows[p][-1] + bits[p][k] * half)
+    halves = [pl.ds(h * (EMBED // 2), EMBED // 2) for h in range(2)]
     sent = []
+
+    def scatter_copy(k, p, h):
+        half = (128, 64, 32)[k]
+        src = pl.multiple_of(lows[p][k] + (1 - bits[p][k]) * half, 32)
+        return pltpu.make_async_remote_copy(
+            src_ref=mine.at[pl.ds(src, half), halves[h]], dst_ref=landing.at[p, pl.ds((0, 128, 192)[k], half), halves[h]],
+            send_sem=rs_send.at[k, p, h], recv_sem=rs_recv.at[k, p, h], device_id=(near[PART_DIMS[p][k]],),
+            device_id_type=MESH)
+
+    for h in range(2):
+        for p in range(3):
+            scatter_copy(0, p, h).start()
     for k, half in enumerate((128, 64, 32)):
-        base = (0, 128, 192)[k]
-        copies = []
-        for p in range(3):
-            d = PART_DIMS[p][k]
-            bit = (chip // d) % 2
-            src = pl.multiple_of(lows[p] + (1 - bit) * half, 32)
-            copies.append(pltpu.make_async_remote_copy(
-                src_ref=mine.at[pl.ds(src, half)], dst_ref=landing.at[p, pl.ds(base, half)],
-                send_sem=rs_send.at[k, p], recv_sem=rs_recv.at[k, p], device_id=(near[d],), device_id_type=MESH))
-            copies[-1].start()
-        kept.append(list(lows))
-        for p in range(3):
-            bit = (chip // PART_DIMS[p][k]) % 2
-            lows[p] = lows[p] + bit * half
-            copies[p].wait_recv()
-            rows = pl.ds(pl.multiple_of(lows[p], 32), half)
-            total = mine[rows, :] + landing[p, base:base + half, :]
-            if k < 2:
-                mine[rows, :] = total
-            else:
-                full[core, rows, :] = total
-        sent += copies
-
-    def share(low, size, p, k):
+        for h in range(2):
+            for p in range(3):
+                scatter_copy(k, p, h).wait_recv()
+                rows = pl.ds(pl.multiple_of(lows[p][k + 1], 32), half)
+                base = (0, 128, 192)[k]
+                total = mine[rows, halves[h]] + landing[p, base:base + half, halves[h]]
+                if k < 2:
+                    mine[rows, halves[h]] = total
+                    scatter_copy(k + 1, p, h).start()
+                else:
+                    full[core, rows, halves[h]] = total
+                sent.append(scatter_copy(k, p, h))
+
+    def share(low, size, p, k, h):
         rows = pl.ds(pl.multiple_of(low, 32), size)
         return pltpu.make_async_remote_copy(
-            src_ref=full.at[core, rows], dst_ref=full.at[core, rows], send_sem=out_send.at[p, k],
-            recv_sem=out_recv.at[p, k], device_id=(other_core,), device_id_type=MESH)
+            src_ref=full.at[core, rows, halves[h]], dst_ref=full.at[core, rows, halves[h]], send_sem=out_send.at[p, k, h],
+            recv_sem=out_recv.at[p, k, h], device_id=(other_core,), device_id_type=MESH)
+
+    def gather_copy(k, p, h):
+        rows = pl.ds(pl.multiple_of(lows[p][k + 1], 32), (128, 64, 32)[k])
+        return pltpu.make_async_remote_copy(
+            src_ref=full.at[core, rows, halves[h]], dst_ref=full.at[core, rows, halves[h]], send_sem=ag_send.at[k, p, h],
+            recv_sem=ag_recv.at[k, p, h], device_id=(near[PART_DIMS[p][k]],), device_id_type=MESH)
 
     to_core.wait_send()
     pl.semaphore_signal(ready, inc=1, device_id=(other_core,), device_id_type=MESH)
     pl.semaphore_wait(ready, 1)
     shares = []
+    for h in range(2):
+        for p in range(3):
+            gather_copy(2, p, h).start()
+            shares.append(share(lows[p][3], 32, p, 3, h))
+            shares[-1].start()
     for k in (2, 1, 0):
-        size = (128, 64, 32)[k]
-        copies = []
-        for p in range(3):
-            d = PART_DIMS[p][k]
-            rows = pl.ds(pl.multiple_of(lows[p], 32), size)
-            copies.append(pltpu.make_async_remote_copy(
-                src_ref=full.at[core, rows], dst_ref=full.at[core, rows], send_sem=ag_send.at[k, p],
-                recv_sem=ag_recv.at[k, p], device_id=(near[d],), device_id_type=MESH))
-            copies[-1].start()
-        if k == 2:
+        for h in range(2):
             for p in range(3):
-                shares.append(share(lows[p], size, p, 3))
+                size = (128, 64, 32)[k]
+                gather_copy(k, p, h).wait_recv()
+                if k > 0:
+                    gather_copy(k - 1, p, h).start()
+                shares.append(share(lows[p][k] + (1 - bits[p][k]) * size, size, p, k, h))
                 shares[-1].start()
-        for p in range(3):
-            bit = (chip // PART_DIMS[p][k]) % 2
-            copies[p].wait_recv()
-            shares.append(share(kept[k][p] + (1 - bit) * size, size, p, k))
-            shares[-1].start()
-            lows[p] = kept[k][p]
-        sent += copies
+                sent.append(gather_copy(k, p, h))
     write_mine = [pltpu.make_async_copy(full.at[a], ref, load_sem.at[a, 0]) for a, ref in ((0, dw_img_ref), (1, dw_txt_ref))]
     for c in stat_copies:
         c.wait_recv()
@@ -385,7 +371,7 @@
             out_specs=[hbm, hbm, vmem],
             scratch_shapes=[
                 pltpu.VMEM((2, 9, ROWS, EMBED), BF16),
-                pltpu.VMEM((9, 1, ROWS), jnp.int32),
+                pltpu.VMEM((8, 1, ROWS), jnp.int32), pltpu.VMEM((9, 1, ROWS), jnp.int32),
                 pltpu.VMEM((2 * ROWS, 128), jnp.int32),
                 pltpu.VMEM((2, 2 * ROWS, EMBED), F32),
                 pltpu.VMEM((2, ROWS, EMBED), F32),
@@ -410,7 +396,8 @@
                 pltpu.VMEM((2, ROWS, EMBED), F32), pltpu.VMEM((ROWS, EMBED), BF16),
                 pltpu.VMEM((EMBED, EMBED), F32), pltpu.VMEM((2, EMBED, EMBED), F32), pltpu.VMEM((EMBED, EMBED), F32),
                 pltpu.VMEM((3, 224, EMBED), F32), pltpu.VMEM((16, 4, 8, 128), F32),
-                dma((2, 3)), dma, dma, dma((3, 3)), dma((3, 3)), dma((3, 3)), dma((3, 3)), dma((3, 4)), dma((3, 4)),
+                dma((2, 3)), dma, dma, dma((3, 3, 2)), dma((3, 3, 2)), dma((3, 3, 2)), dma((3, 3, 2)), dma((3, 4, 2)),
+                dma((3, 4, 2)),
                 dma((15,)), dma((15,)), pltpu.SemaphoreType.REGULAR,
             ],
             compiler_params=pltpu.CompilerParams(

time: 286 us -> 263 us (0.920)
  Pallas kernels: 269 us -> 247 us
    pallas_call x1, Pallas kernels: 209 us -> 190 us  [local_fn(): pl.pallas_call(pair_kernel, out_shape=[jax.ShapeDtypeStruct((ROWS, EMBED)...]
    pallas_call x1, Pallas kernels: 60.4 us -> 56.5 us  [local_fn(): pl.pallas_call(tail_kernel, out_shape=[jax.ShapeDtypeStruct((EMBED, EMBED...]
where the time goes in v3:
time: 263 us
  Pallas kernels  247 us (94%)
  between operations  7.98 us (3%)
  local copies, waits for them, and re-layouts  7.68 us (3%)
    pallas_call x1, Pallas kernels, local_fn(): pl.pallas_call(pair_kernel, out_shape=[jax.ShapeDtypeStruct((ROWS, EMBED)...  190 us
    pallas_call x1, Pallas kernels, local_fn(): pl.pallas_call(tail_kernel, out_shape=[jax.ShapeDtypeStruct((EMBED, EMBED...  56.5 us

profile of v3, /device:TPU:1, one launch (start us, length us, event | category | flops | bytes accessed | tf_op | source)
XLA Modules:
  0.0 263.0 jit_solution(12253061105219701420)
XLA Ops:
  2.0 0.6 pad_maximum_fusion.scal_ref
  2.5 1.7 broadcast_in_dim.2.idrow_ref
  4.2 190.2 %shard_map.110 = (f32[1024,768]{1,0:T(8,128)}, f32[1024,768]{1,0:T(8,128)}, f32[4,8,128]{2,1,0:T(8,128)}) custom-call(f32[2]{0:T(128)} %pad_maximum_fusion.scal_ref, bf16[1024,768]{1,0:T(8,128)(2,1)} %feat_img.3, bf16[1024,768]{1,0:T(8,128)(2,1)} %feat_txt.3, bf16[768,768]{1,0:T(8,128)(2,1)} %w_img.3, bf16[768,768]{1,0:T(8,128)(2,1)} %w_txt.3, ...), custom_call_target="tpu_custom_call" | custom-call | flops 109999996928 | bytes 16000000 | tf_op jit(solution)/shard_map/pallas_call | solution.py:367
  194.5 56.5 %shard_map.111 = (f32[768,768]{1,0:T(8,128)}, f32[768,768]{1,0:T(8,128)}, f32[4,8,128]{2,1,0:T(8,128)}) custom-call(f32[2]{0:T(128)} %pad_maximum_fusion.scal_ref, bf16[1024,768]{1,0:T(8,128)(2,1)} %feat_img.3, bf16[1024,768]{1,0:T(8,128)(2,1)} %feat_txt.3, bf16[768,768]{1,0:T(8,128)(2,1)} %w_img.3, bf16[768,768]{1,0:T(8,128)(2,1)} %w_txt.3, ...), custom_call_target="tpu_custom_call" | custom-call | flops 5000000000 | bytes 16000000 | tf_op jit(solution)/shard_map/pallas_call | solution.py:389
  251.0 1.2 fusion
  254.8 0.0 copy-start
  254.9 3.4 %copy.16 = f32[768,768]{1,0:T(8,128)} copy(f32[768,768]{1,0:T(8,128)} %get-tuple-element.29) | data formatting | bytes 4718592
  258.2 0.0 copy-done
  258.2 1.4 copy.17
Async XLA Ops:
  254.8 3.4 %copy-start = (f32[768,768]{1,0:T(8,128)S(1)}, f32[768,768]{1,0:T(8,128)}, u32[]{:S(2)}) copy-start(f32[768,768]{1,0:T(8,128)} %get-tuple-element.30) | copy-start | bytes 7077892

commit v4 on v3

v4 whole, which is shorter than its diff:
```python
import jax
import jax.numpy as jnp
from jax import lax
from jax.experimental import pallas as pl
from jax.experimental.pallas import tpu as pltpu
from jax.sharding import PartitionSpec as P

F32, BF16 = jnp.float32, jnp.bfloat16
MESH = pl.DeviceIdType.MESH
ROWS, EMBED = 1024, 768
TILE_M, CHUNK_R = 512, 16
LOG2E = 1.4426950408889634
CONTRACT_ROWS = (((0,), (0,)), ((), ()))
CONTRACT_COLS = (((1,), (1,)), ((), ()))

PART_ROWS = ((0, 352), (352, 336), (688, 336))
PART_DIMS = ((1, 2, 4), (2, 4, 1), (4, 1, 2))


def turn_rel(turn, part):
    dims = PART_DIMS[part]
    return {0: dims[0], 1: dims[1], 2: dims[2], 3: dims[0] | dims[1], 4: dims[0] | dims[2], 5: dims[1] | dims[2],
            6: 7}[turn]


SLOT = {(part, turn_rel(turn, part)): 2 + turn for turn in range(7) for part in range(3)}
SLOT.update({(part, 0): 0 for part in range(3)})


def turn_sends(turn):
    ways = {-1: ((None, 0), (None, 1), (None, 2)), 0: ((0, 1), (0, 2)), 1: ((1, 2),), 3: ((3, 2),)}.get(turn, ())
    return [(p, 0 if turn < 0 else turn_rel(turn, p), PART_DIMS[p][k]) for _, k in ways for p in range(3)]


def pair_kernel(scal_ref, feat_img, feat_txt, w_img, w_txt, ids_ref, idrow_ref, dw_img_ref, dw_txt_ref, tot_ref,
                slots, ids_raw, ids_all, id_rows, acc, partner, s0, s1, g0, g1, sums, stats,
                send_sem, recv_sem, ids_send, ids_recv, pair_send, pair_recv, grad_send, grad_recv, load_sem,
                late_sem, core_send, core_recv, rs_send, rs_recv, ag_send, ag_recv, out_send, out_recv, st_send, st_recv, ready):
    me = lax.axis_index("data")
    core = me % 2
    chip = me // 2

    def peer(rel):
        where = chip
        for d in (1, 2, 4):
            if rel & d:
                where = where + d * (1 - 2 * ((chip // d) % 2))
        return where * 2 + core

    other_core = chip * 2 + (1 - core)
    loads = [pltpu.make_async_copy(src, slots.at[a, 8], load_sem.at[2 * a]) for a, src in ((0, feat_txt), (1, feat_img))]
    loads += [pltpu.make_async_copy(src, slots.at[a, 7, pl.ds(0, EMBED)], load_sem.at[2 * a + 1])
              for a, src in ((0, w_txt), (1, w_img))]
    loads.append(pltpu.make_async_copy(ids_ref, ids_raw.at[0], load_sem.at[4]))
    loads.append(pltpu.make_async_copy(idrow_ref, id_rows.at[pl.ds(0, ROWS)], load_sem.at[5]))
    for c in loads:
        c.start()
    acc[...] = jnp.zeros_like(acc)
    sums[...] = jnp.zeros_like(sums)
    for c in loads:
        c.wait()

    def embed(i, carry):
        a, rows = i // 2, pl.ds(pl.multiple_of((i % 2) * (ROWS // 2), ROWS // 2), ROWS // 2)
        raw = jnp.dot(slots[a, 8, rows, :], slots[a, 7, 0:EMBED, :], preferred_element_type=F32)
        slots[a, 0, rows, :] = (raw * lax.rsqrt(jnp.sum(raw * raw, axis=1, keepdims=True))).astype(BF16)
        return carry

    lax.fori_loop(0, 4, embed, 0)

    barrier = pltpu.get_barrier_semaphore()
    others = [(me + k) % 16 for k in range(1, 16)]
    for dev in others:
        pl.semaphore_signal(barrier, inc=1, device_id=(dev,), device_id_type=MESH)
    pl.semaphore_wait(barrier, len(others))

    def part_copy(a, p, rel, d):
        lo, size = PART_ROWS[p]
        return pltpu.make_async_remote_copy(
            src_ref=slots.at[a, SLOT[p, rel], pl.ds(lo, size)],
            dst_ref=slots.at[a, SLOT[p, rel ^ d], pl.ds(lo, size)],
            send_sem=send_sem.at[a, p, SLOT[p, rel ^ d]],
            recv_sem=recv_sem.at[a, p, SLOT[p, rel ^ d]],
            device_id=(peer(d),), device_id_type=MESH)

    def arrival(a, p, rel):
        d = next(x for x in reversed(PART_DIMS[p]) if rel & x)
        part_copy(a, p, rel ^ d, d).wait_recv()

    pair_copies = [pltpu.make_async_remote_copy(
        src_ref=slots.at[a, 0], dst_ref=slots.at[a, 1], send_sem=pair_send.at[a], recv_sem=pair_recv.at[a],
        device_id=(other_core,), device_id_type=MESH) for a in range(2)]
    pair_copies.append(pltpu.make_async_remote_copy(
        src_ref=id_rows.at[pl.ds(0, ROWS)], dst_ref=id_rows.at[pl.ds(ROWS, ROWS)], send_sem=pair_send.at[2],
        recv_sem=pair_recv.at[2], device_id=(other_core,), device_id_type=MESH))
    id_copies = []
    for rel in range(1, 8):
        id_copies.append(pltpu.make_async_remote_copy(
            src_ref=ids_raw.at[0], dst_ref=ids_raw.at[rel], send_sem=ids_send.at[rel],
            recv_sem=ids_recv.at[rel], device_id=(peer(rel),), device_id_type=MESH))
    for c in id_copies:
        c.start()
    for c in pair_copies[::-1]:
        c.start()
    for send in turn_sends(-1):
        part_copy(0, *send).start()

    scale, bias = scal_ref[0], scal_ref[1]
    for c in id_copies:
        c.wait_recv()
    lane = lax.broadcasted_iota(jnp.int32, (1, ROWS), 1)
    ids_all[0] = ids_raw[0]
    for turn in range(7):
        ids_all[2 + turn] = jnp.where(
            lane < PART_ROWS[1][0], ids_raw[turn_rel(turn, 0)],
            jnp.where(lane < PART_ROWS[2][0], ids_raw[turn_rel(turn, 1)], ids_raw[turn_rel(turn, 2)]))
    for c in pair_copies:
        c.wait_recv()

    n_m = 2 * ROWS // TILE_M

    def slot_of(block):
        return block + (block + 7) // 8

    def row_tile(t):
        return (t % n_m + (n_m // 2) * ((t // n_m + 7) // 8)) % n_m

    def scores(a, t, s_ref):
        m, slot = pl.multiple_of(row_tile(t) * TILE_M, TILE_M), slot_of(t // n_m)
        rows = slots[1 - a, m // ROWS, pl.ds(pl.multiple_of(m % ROWS, TILE_M), TILE_M), :]
        s_ref[...] = lax.dot_general(rows, slots[a, slot], CONTRACT_COLS, preferred_element_type=F32)

    def tile_grad(a, t, s_ref, g_ref):
        m, slot = pl.multiple_of(row_tile(t) * TILE_M, TILE_M), slot_of(t // n_m)

        col_ids = ids_all[slot]

        def rows_step(i, carry):
            x0, x1 = carry
            top = pl.multiple_of(i * CHUNK_R, CHUNK_R)
            row_ids = jnp.concatenate([id_rows[pl.ds(pl.multiple_of(m + top, CHUNK_R), CHUNK_R), :]] * 8, axis=1)
            sim = s_ref[pl.ds(top, CHUNK_R), :]
            sign = jnp.where(row_ids == col_ids, -1.0, 1.0)
            margin = sign * (scale * sim + bias)
            e = jnp.exp2(jnp.abs(margin) * (-LOG2E))
            d = 1.0 + e
            r = 1.0 / d
            grad = sign * jnp.where(margin >= 0, r, e * r)
            g_ref[pl.ds(top, CHUNK_R), :] = grad.astype(BF16)
            if a == 0:
                return x0 + jnp.maximum(margin, 0.0), x1 * d + e
            return x0 + grad * sim, x1 + grad

        x1 = jnp.zeros((CHUNK_R, ROWS), F32) if a == 0 else sums[3]
        x0, x1 = lax.fori_loop(0, TILE_M // CHUNK_R, rows_step, (sums[2 * a], x1), unroll=True)
        sums[2 * a] = x0
        sums[2 * a + 1] = sums[1] + jnp.log1p(x1) if a == 0 else x1

    def row_grad(a, t, g_ref):
        m, slot = pl.multiple_of(row_tile(t) * TILE_M, TILE_M), slot_of(t // n_m)
        acc[1 - a, pl.ds(m, TILE_M), :] += jnp.dot(g_ref[...], slots[a, slot], preferred_element_type=F32)

    def run_turn(a, turn):
        for p in range(3):
            arrival(a, p, turn_rel(turn, p))
        for send in turn_sends(turn):
            part_copy(a, *send).start()
        if (a, turn) == (0, 3):
            for send in turn_sends(-1):
                part_copy(1, *send).start()

    grad_copies = [pltpu.make_async_remote_copy(
        src_ref=acc.at[x, pl.ds(ROWS, ROWS)], dst_ref=partner.at[x], send_sem=grad_send.at[x],
        recv_sem=grad_recv.at[x], device_id=(other_core,), device_id_type=MESH) for x in range(2)]

    def stream(a):
        t0, t_end = 0, 8 * n_m
        scores(a, t0, s0)
        scores(a, t0 + 1, s1)
        tile_grad(a, t0, s0, g0)

        def body(k, carry):
            t = t0 + 2 * k + 1
            for task, todo in actions[a].items():
                @pl.when(t + 1 == task)
                def _():
                    for act in todo:
                        act()
            scores(a, t + 1, s0)
            tile_grad(a, t, s1, g1)
            row_grad(a, t - 1, g0)
            scores(a, t + 2, s1)
            tile_grad(a, t + 1, s0, g0)
            row_grad(a, t, g1)
            return carry

        lax.fori_loop(0, (t_end - t0 - 2) // 2, body, 0)
        grad_copies[1 - a].start()
        tile_grad(a, t_end - 1, s1, g1)
        row_grad(a, t_end - 2, g0)
        row_grad(a, t_end - 1, g1)

    half_rows = EMBED // 2
    steps = (64, 32, 16)
    bits = [[(chip // PART_DIMS[p][k]) % 2 for k in range(3)] for p in range(3)]
    lows = [[core * half_rows + 128 * p] for p in range(3)]
    for p in range(3):
        for k in range(3):
            lows[p].append(lows[p][-1] + bits[p][k] * steps[k])
    cols = [pl.ds(h * (EMBED // 2), EMBED // 2) for h in range(2)]
    lanes = [(p, h) for h in range(2) for p in range(3)]
    started = []

    def start(make, *args):
        make(*args).start()
        started.append((make, args))

    def rows_at(low, size, base=0):
        return pl.ds(pl.multiple_of(low + base, 16), size)

    def near(p, k):
        return (peer(PART_DIMS[p][k]),)

    def core_copy(x):
        return pltpu.make_async_remote_copy(
            src_ref=acc.at[x, rows_at((1 - core) * half_rows, half_rows, ROWS)], dst_ref=partner.at[x, pl.ds(0, half_rows)],
            send_sem=core_send.at[x], recv_sem=core_recv.at[x], device_id=(other_core,), device_id_type=MESH)

    def scatter_copy(x, k, p, h):
        return pltpu.make_async_remote_copy(
            src_ref=acc.at[x, rows_at(lows[p][k] + (1 - bits[p][k]) * steps[k], steps[k], ROWS), cols[h]],
            dst_ref=partner.at[x, pl.ds(half_rows + 112 * p + (0, 64, 96)[k], steps[k]), cols[h]],
            send_sem=rs_send.at[x, k, p, h], recv_sem=rs_recv.at[x, k, p, h], device_id=near(p, k), device_id_type=MESH)

    def gather_copy(x, k, p, h):
        rows = rows_at(lows[p][k + 1], steps[k])
        return pltpu.make_async_remote_copy(
            src_ref=acc.at[x, rows, cols[h]], dst_ref=acc.at[x, rows, cols[h]], send_sem=ag_send.at[x, k, p, h],
            recv_sem=ag_recv.at[x, k, p, h], device_id=near(p, k), device_id_type=MESH)

    def share(x, k, p, h):
        rows = rows_at(lows[p][3], 16) if k == 3 else rows_at(lows[p][k] + (1 - bits[p][k]) * steps[k], steps[k])
        return pltpu.make_async_remote_copy(
            src_ref=acc.at[x, rows, cols[h]], dst_ref=acc.at[x, rows, cols[h]], send_sem=out_send.at[x, k, p, h],
            recv_sem=out_recv.at[x, k, p, h], device_id=(other_core,), device_id_type=MESH)

    def late_load(x):
        srcs = ((feat_txt, slots.at[0, 5]), (w_txt, slots.at[0, 6, pl.ds(0, EMBED)])) if x == 0 else (
            (feat_img, slots.at[0, 2]), (w_img, slots.at[0, 3, pl.ds(0, EMBED)]))
        return [pltpu.make_async_copy(src, dst, late_sem.at[x, k]) for k, (src, dst) in enumerate(srcs)]

    def begin_load(x, turns):
        for turn in turns:
            for send in turn_sends(turn):
                part_copy(0, *send).wait_send()
        for c in late_load(x):
            c.start()

    def head_partial(x):
        for c in late_load(x):
            c.wait()
        feat, head = (5, 6) if x == 0 else (2, 3)

        def rows_step(i, carry):
            rows = pl.ds(pl.multiple_of(i * 256, 256), 256)
            raw = jnp.dot(slots[0, feat, rows, :], slots[0, head, 0:EMBED, :], preferred_element_type=F32)
            inv = lax.rsqrt(jnp.sum(raw * raw, axis=1, keepdims=True))
            unit = raw * inv
            grad = scale * ((acc[x, rows, :] + partner[x, rows, :]) * F32(1.0 / (16 * ROWS)))
            slots[0, 4, rows, :] = (inv * (grad - unit * jnp.sum(unit * grad, axis=1, keepdims=True))).astype(BF16)
            return carry

        lax.fori_loop(0, ROWS // 256, rows_step, 0)
        grad_copies[x].wait_send()
        acc[x, ROWS:ROWS + EMBED, :] = lax.dot_general(
            slots[0, feat], slots[0, 4], CONTRACT_ROWS, preferred_element_type=F32)
        for dev in [other_core] + [peer(d) for d in (1, 2, 4)]:
            pl.semaphore_signal(ready.at[x], inc=1, device_id=(dev,), device_id_type=MESH)

    def step_core(x):
        pl.semaphore_wait(ready.at[x], 4)
        start(core_copy, x)

    def step_first(x):
        core_copy(x).wait_recv()
        acc[x, rows_at(core * half_rows, half_rows, ROWS), :] += partner[x, 0:half_rows, :]
        for p, h in lanes:
            start(scatter_copy, x, 0, p, h)

    def step_scatter(x, k):
        for p, h in lanes:
            scatter_copy(x, k, p, h).wait_recv()
            base = half_rows + 112 * p + (0, 64, 96)[k]
            mine = rows_at(lows[p][k + 1], steps[k], ROWS)
            total = acc[x, mine, cols[h]] + partner[x, base:base + steps[k], cols[h]]
            if k < 2:
                acc[x, mine, cols[h]] = total
                start(scatter_copy, x, k + 1, p, h)
            else:
                acc[x, rows_at(lows[p][3], 16), cols[h]] = total
                start(gather_copy, x, 2, p, h)
                start(share, x, 3, p, h)

    def step_gather(x, k):
        for p, h in lanes:
            gather_copy(x, k, p, h).wait_recv()
            if k > 0:
                start(gather_copy, x, k - 1, p, h)
            start(share, x, k, p, h)

    def step_out(x):
        for k in (3, 2, 1, 0):
            for p, h in lanes:
                share(x, k, p, h).wait_recv()
        outs[x].start()

    outs = [pltpu.make_async_copy(acc.at[x, pl.ds(0, EMBED)], ref, load_sem.at[x])
            for x, ref in ((0, dw_txt_ref), (1, dw_img_ref))]
    actions = [{b * n_m: [lambda a=a, b=b: run_turn(a, b - 1)] for b in range(1, 8)} for a in range(2)]
    actions[0][7 * n_m].append(lambda: begin_load(1, (-1, 0, 1)))
    actions[1][n_m].append(lambda: (step_core(1), begin_load(0, (3,))))
    actions[1][5 * n_m].append(lambda: step_first(1))
    actions[1][7 * n_m + 2] = [lambda: step_scatter(1, 0)]

    stream(0)
    grad_copies[1].wait_recv()
    head_partial(1)
    stream(1)
    step_scatter(1, 1)
    for x in range(4):
        rows = sums[x, 0:8, :] + sums[x, 8:16, :]
        stats[me, x] = sum(rows[:, v:v + 128] for v in range(0, ROWS, 128))
    stat_copies = [pltpu.make_async_remote_copy(
        src_ref=stats.at[me], dst_ref=stats.at[me], send_sem=st_send.at[k], recv_sem=st_recv.at[k],
        device_id=(dev,), device_id_type=MESH) for k, dev in enumerate(others)]
    grad_copies[0].wait_recv()
    step_scatter(1, 2)
    head_partial(0)
    for c in stat_copies:
        c.start()
    step_core(0)
    step_gather(1, 2)
    step_first(0)
    step_gather(1, 1)
    step_scatter(0, 0)
    step_gather(1, 0)
    step_scatter(0, 1)
    step_out(1)
    step_scatter(0, 2)
    for c in stat_copies:
        c.wait_recv()
    total = stats[0]
    for dev in range(1, 16):
        total = total + stats[dev]
    tot_ref[...] = jnp.broadcast_to(jnp.sum(jnp.sum(total, axis=1, keepdims=True), axis=2, keepdims=True), (4, 8, 128))
    for k in (2, 1, 0):
        step_gather(0, k)
    step_out(0)
    for c in pair_copies + id_copies + stat_copies:
        c.wait_send()
    for make, args in started:
        make(*args).wait_send()
    for turn in (-1, 0, 1, 3):
        for send in turn_sends(turn):
            part_copy(1, *send).wait_send()
    for c in outs:
        c.wait()


def solution(mesh):
    n_dev = mesh.shape["data"]

    def local_fn(feat_img, feat_txt, w_img, w_txt, log_temp, logit_bias, pair_ids):
        total_rows = feat_img.shape[0] * n_dev
        temp_scale = jnp.exp(log_temp)
        scal = jnp.stack([temp_scale, logit_bias])
        vmem = pl.BlockSpec(memory_space=pltpu.VMEM)
        smem = pl.BlockSpec(memory_space=pltpu.SMEM)
        hbm = pl.BlockSpec(memory_space=pl.ANY)
        dma = pltpu.SemaphoreType.DMA
        dw_img, dw_txt, totals = pl.pallas_call(
            pair_kernel,
            out_shape=[jax.ShapeDtypeStruct((EMBED, EMBED), F32)] * 2 + [jax.ShapeDtypeStruct((4, 8, 128), F32)],
            in_specs=[smem] + [hbm] * 6,
            out_specs=[hbm, hbm, vmem],
            scratch_shapes=[
                pltpu.VMEM((2, 9, ROWS, EMBED), BF16),
                pltpu.VMEM((8, 1, ROWS), jnp.int32), pltpu.VMEM((9, 1, ROWS), jnp.int32),
                pltpu.VMEM((2 * ROWS, 128), jnp.int32),
                pltpu.VMEM((2, 2 * ROWS, EMBED), F32),
                pltpu.VMEM((2, ROWS, EMBED), F32),
                pltpu.VMEM((TILE_M, ROWS), F32), pltpu.VMEM((TILE_M, ROWS), F32),
                pltpu.VMEM((TILE_M, ROWS), BF16), pltpu.VMEM((TILE_M, ROWS), BF16),
                pltpu.VMEM((4, CHUNK_R, ROWS), F32), pltpu.VMEM((16, 4, 8, 128), F32),
                dma((2, 3, 9)), dma((2, 3, 9)), dma((9,)), dma((9,)), dma((3,)), dma((3,)), dma((2,)), dma((2,)),
                dma((6,)), dma((2, 2)), dma((2,)), dma((2,)), dma((2, 3, 3, 2)), dma((2, 3, 3, 2)), dma((2, 3, 3, 2)),
                dma((2, 3, 3, 2)), dma((2, 4, 3, 2)), dma((2, 4, 3, 2)), dma((15,)), dma((15,)),
                pltpu.SemaphoreType.REGULAR((2,)),
            ],
            compiler_params=pltpu.CompilerParams(
                collective_id=0, has_side_effects=True, vmem_limit_bytes=66_000_000),
            cost_estimate=pl.CostEstimate(flops=110_000_000_000, bytes_accessed=16_000_000, transcendentals=0),
        )(scal, feat_img, feat_txt, w_img, w_txt, pair_ids.reshape(1, ROWS),
          jnp.broadcast_to(pair_ids[:, None], (ROWS, 128)))
        loss_sum, temp_sum, bias_sum = totals[0, 0, 0] + totals[1, 0, 0], totals[2, 0, 0], totals[3, 0, 0]
        return loss_sum / total_rows, temp_scale * (temp_sum / total_rows), bias_sum / total_rows, dw_img, dw_txt

    return jax.shard_map(
        local_fn,
        mesh=mesh,
        in_specs=(P("data", None), P("data", None), P(None, None), P(None, None), P(), P(), P("data")),
        out_specs=(P(), P(), P(), P(None, None), P(None, None)),
        check_vma=False,
    )
```

time: 263 us -> 247 us (0.939)
  Pallas kernels: 247 us -> 231 us
    pallas_call x2 -> x1, Pallas kernels: 247 us -> 231 us  [local_fn(): pl.pallas_call(pair_kernel, out_shape=[jax.ShapeDtypeStruct((EMBED, EMBED...]
where the time goes in v4:
time: 247 us
  Pallas kernels  231 us (94%)
  between operations  7.97 us (3%)
  local copies, waits for them, and re-layouts  7.68 us (3%)
    pallas_call x1, Pallas kernels, local_fn(): pl.pallas_call(pair_kernel, out_shape=[jax.ShapeDtypeStruct((EMBED, EMBED...  231 us

profile of v4, /device:TPU:1, one launch (start us, length us, event | category | flops | bytes accessed | tf_op | source)
XLA Modules:
  0.0 247.0 jit_solution(5711616140507871806)
XLA Ops:
  2.0 0.6 pad_maximum_fusion.scal_ref
  2.5 1.7 broadcast_in_dim.2.idrow_ref
  4.2 230.7 %shard_map.110 = (f32[768,768]{1,0:T(8,128)}, f32[768,768]{1,0:T(8,128)}, f32[4,8,128]{2,1,0:T(8,128)}) custom-call(f32[2]{0:T(128)} %pad_maximum_fusion.scal_ref, bf16[1024,768]{1,0:T(8,128)(2,1)} %feat_img.1, bf16[1024,768]{1,0:T(8,128)(2,1)} %feat_txt.1, bf16[768,768]{1,0:T(8,128)(2,1)} %w_img.1, bf16[768,768]{1,0:T(8,128)(2,1)} %w_txt.1, ...), custom_call_target="tpu_custom_call" | custom-call | flops 109999996928 | bytes 16000000 | tf_op jit(solution)/shard_map/pallas_call | solution.py:381
  235.0 1.2 fusion
  238.8 0.0 copy-start
  238.8 3.4 %copy.16 = f32[768,768]{1,0:T(8,128)} copy(f32[768,768]{1,0:T(8,128)} %get-tuple-element.23) | data formatting | bytes 4718592
  242.2 0.0 copy-done
  242.2 1.4 copy.17
Async XLA Ops:
  238.8 3.4 %copy-start = (f32[768,768]{1,0:T(8,128)S(1)}, f32[768,768]{1,0:T(8,128)}, u32[]{:S(2)}) copy-start(f32[768,768]{1,0:T(8,128)} %get-tuple-element.24) | copy-start | bytes 7077892

commit v5 on v4

--- a/solution.py
+++ b/solution.py
@@ -27,13 +27,17 @@
 SLOT.update({(part, 0): 0 for part in range(3)})
 
 
+def own_sends(k):
+    return [(p, 0, PART_DIMS[p][k]) for p in range(3)]
+
+
 def turn_sends(turn):
     ways = {-1: ((None, 0), (None, 1), (None, 2)), 0: ((0, 1), (0, 2)), 1: ((1, 2),), 3: ((3, 2),)}.get(turn, ())
     return [(p, 0 if turn < 0 else turn_rel(turn, p), PART_DIMS[p][k]) for _, k in ways for p in range(3)]
 
 
 def pair_kernel(scal_ref, feat_img, feat_txt, w_img, w_txt, ids_ref, idrow_ref, dw_img_ref, dw_txt_ref, tot_ref,
-                slots, ids_raw, ids_all, id_rows, acc, partner, s0, s1, g0, g1, sums, stats,
+                slots, ids_raw, ids_all, id_rows, acc, partner, s0, s1, g0, g1, sums, stats, head,
                 send_sem, recv_sem, ids_send, ids_recv, pair_send, pair_recv, grad_send, grad_recv, load_sem,
                 late_sem, core_send, core_recv, rs_send, rs_recv, ag_send, ag_recv, out_send, out_recv, st_send, st_recv, ready):
     me = lax.axis_index("data")
@@ -48,25 +52,28 @@
         return where * 2 + core
 
     other_core = chip * 2 + (1 - core)
-    loads = [pltpu.make_async_copy(src, slots.at[a, 8], load_sem.at[2 * a]) for a, src in ((0, feat_txt), (1, feat_img))]
-    loads += [pltpu.make_async_copy(src, slots.at[a, 7, pl.ds(0, EMBED)], load_sem.at[2 * a + 1])
-              for a, src in ((0, w_txt), (1, w_img))]
-    loads.append(pltpu.make_async_copy(ids_ref, ids_raw.at[0], load_sem.at[4]))
-    loads.append(pltpu.make_async_copy(idrow_ref, id_rows.at[pl.ds(0, ROWS)], load_sem.at[5]))
-    for c in loads:
+    txt_loads = [pltpu.make_async_copy(feat_txt, slots.at[0, 8], load_sem.at[0]),
+                 pltpu.make_async_copy(w_txt, slots.at[0, 7, pl.ds(0, EMBED)], load_sem.at[1])]
+    img_loads = [pltpu.make_async_copy(feat_img.at[pl.ds(0, TILE_M)], g0.at[:, pl.ds(0, EMBED)], load_sem.at[2]),
+                 pltpu.make_async_copy(feat_img.at[pl.ds(TILE_M, TILE_M)], g1.at[:, pl.ds(0, EMBED)], load_sem.at[3]),
+                 pltpu.make_async_copy(w_img, head, load_sem.at[4]),
+                 pltpu.make_async_copy(ids_ref, ids_raw.at[0], load_sem.at[5]),
+                 pltpu.make_async_copy(idrow_ref, id_rows.at[pl.ds(0, ROWS)], load_sem.at[6])]
+    for c in txt_loads + img_loads:
         c.start()
-    acc[...] = jnp.zeros_like(acc)
-    sums[...] = jnp.zeros_like(sums)
-    for c in loads:
+    for c in txt_loads:
         c.wait()
 
-    def embed(i, carry):
-        a, rows = i // 2, pl.ds(pl.multiple_of((i % 2) * (ROWS // 2), ROWS // 2), ROWS // 2)
-        raw = jnp.dot(slots[a, 8, rows, :], slots[a, 7, 0:EMBED, :], preferred_element_type=F32)
-        slots[a, 0, rows, :] = (raw * lax.rsqrt(jnp.sum(raw * raw, axis=1, keepdims=True))).astype(BF16)
+    def unit_rows(feat_rows, weights):
+        raw = jnp.dot(feat_rows, weights, preferred_element_type=F32)
+        return (raw * lax.rsqrt(jnp.sum(raw * raw, axis=1, keepdims=True))).astype(BF16)
+
+    def embed_txt(i, carry):
+        rows = pl.ds(pl.multiple_of(i * TILE_M, TILE_M), TILE_M)
+        slots[0, 0, rows, :] = unit_rows(slots[0, 8, rows, :], slots[0, 7, 0:EMBED, :])
         return carry
 
-    lax.fori_loop(0, 4, embed, 0)
+    lax.fori_loop(0, ROWS // TILE_M, embed_txt, 0)
 
     barrier = pltpu.get_barrier_semaphore()
     others = [(me + k) % 16 for k in range(1, 16)]
@@ -98,11 +105,20 @@
         id_copies.append(pltpu.make_async_remote_copy(
             src_ref=ids_raw.at[0], dst_ref=ids_raw.at[rel], send_sem=ids_send.at[rel],
             recv_sem=ids_recv.at[rel], device_id=(peer(rel),), device_id_type=MESH))
+    pair_copies[0].start()
+    for send in own_sends(0):
+        part_copy(0, *send).start()
+    for c in img_loads:
+        c.wait()
     for c in id_copies:
         c.start()
-    for c in pair_copies[::-1]:
+    slots[1, 0, 0:TILE_M, :] = unit_rows(g0[:, 0:EMBED], head[...])
+    slots[1, 0, TILE_M:ROWS, :] = unit_rows(g1[:, 0:EMBED], head[...])
+    acc[...] = jnp.zeros_like(acc)
+    sums[...] = jnp.zeros_like(sums)
+    for c in pair_copies[1:]:
         c.start()
-    for send in turn_sends(-1):
+    for send in own_sends(1):
         part_copy(0, *send).start()
 
     scale, bias = scal_ref[0], scal_ref[1]
@@ -163,17 +179,20 @@
     def run_turn(a, turn):
         for p in range(3):
             arrival(a, p, turn_rel(turn, p))
+        if (a, turn) == (0, 0):
+            for send in own_sends(2):
+                part_copy(0, *send).start()
         for send in turn_sends(turn):
             part_copy(a, *send).start()
-        if (a, turn) == (0, 3):
-            for send in turn_sends(-1):
+        if a == 0 and 3 <= turn <= 5:
+            for send in own_sends(turn - 3):
                 part_copy(1, *send).start()
 
     grad_copies = [pltpu.make_async_remote_copy(
         src_ref=acc.at[x, pl.ds(ROWS, ROWS)], dst_ref=partner.at[x], send_sem=grad_send.at[x],
         recv_sem=grad_recv.at[x], device_id=(other_core,), device_id_type=MESH) for x in range(2)]
 
-    def stream(a):
+    def stream(a, after_loop=lambda: None, near_end=lambda: None):
         t0, t_end = 0, 8 * n_m
         scores(a, t0, s0)
         scores(a, t0 + 1, s1)
@@ -196,8 +215,10 @@
 
         lax.fori_loop(0, (t_end - t0 - 2) // 2, body, 0)
         grad_copies[1 - a].start()
+        after_loop()
         tile_grad(a, t_end - 1, s1, g1)
         row_grad(a, t_end - 2, g0)
+        near_end()
         row_grad(a, t_end - 1, g1)
 
     half_rows = EMBED // 2
@@ -256,14 +277,14 @@
         for c in late_load(x):
             c.start()
 
-    def head_partial(x):
+    def head_partial(x, between=lambda: None):
         for c in late_load(x):
             c.wait()
-        feat, head = (5, 6) if x == 0 else (2, 3)
+        feat, weights = (5, 6) if x == 0 else (2, 3)
 
         def rows_step(i, carry):
             rows = pl.ds(pl.multiple_of(i * 256, 256), 256)
-            raw = jnp.dot(slots[0, feat, rows, :], slots[0, head, 0:EMBED, :], preferred_element_type=F32)
+            raw = jnp.dot(slots[0, feat, rows, :], slots[0, weights, 0:EMBED, :], preferred_element_type=F32)
             inv = lax.rsqrt(jnp.sum(raw * raw, axis=1, keepdims=True))
             unit = raw * inv
             grad = scale * ((acc[x, rows, :] + partner[x, rows, :]) * F32(1.0 / (16 * ROWS)))
@@ -272,14 +293,19 @@
 
         lax.fori_loop(0, ROWS // 256, rows_step, 0)
         grad_copies[x].wait_send()
-        acc[x, ROWS:ROWS + EMBED, :] = lax.dot_general(
-            slots[0, feat], slots[0, 4], CONTRACT_ROWS, preferred_element_type=F32)
         for dev in [other_core] + [peer(d) for d in (1, 2, 4)]:
             pl.semaphore_signal(ready.at[x], inc=1, device_id=(dev,), device_id_type=MESH)
-
-    def step_core(x):
+        between()
+
+        def half_grad(which):
+            cut = pl.ds(pl.multiple_of(which * half_rows, half_rows), half_rows)
+            acc[x, rows_at(which * half_rows, half_rows, ROWS), :] = lax.dot_general(
+                slots[0, feat, :, cut], slots[0, 4], CONTRACT_ROWS, preferred_element_type=F32)
+
+        half_grad(1 - core)
         pl.semaphore_wait(ready.at[x], 4)
         start(core_copy, x)
+        half_grad(core)
 
     def step_first(x):
         core_copy(x).wait_recv()
@@ -318,30 +344,25 @@
             for x, ref in ((0, dw_txt_ref), (1, dw_img_ref))]
     actions = [{b * n_m: [lambda a=a, b=b: run_turn(a, b - 1)] for b in range(1, 8)} for a in range(2)]
     actions[0][7 * n_m].append(lambda: begin_load(1, (-1, 0, 1)))
-    actions[1][n_m].append(lambda: (step_core(1), begin_load(0, (3,))))
-    actions[1][5 * n_m].append(lambda: step_first(1))
+    actions[1][n_m].append(lambda: begin_load(0, (3,)))
+    actions[1][4 * n_m].append(lambda: (grad_copies[1].wait_recv(), head_partial(1)))
+    actions[1][7 * n_m].append(lambda: step_first(1))
     actions[1][7 * n_m + 2] = [lambda: step_scatter(1, 0)]
 
     stream(0)
-    grad_copies[1].wait_recv()
-    head_partial(1)
-    stream(1)
-    step_scatter(1, 1)
+    stream(1, after_loop=lambda: step_scatter(1, 1), near_end=lambda: step_scatter(1, 2))
     for x in range(4):
         rows = sums[x, 0:8, :] + sums[x, 8:16, :]
         stats[me, x] = sum(rows[:, v:v + 128] for v in range(0, ROWS, 128))
     stat_copies = [pltpu.make_async_remote_copy(
         src_ref=stats.at[me], dst_ref=stats.at[me], send_sem=st_send.at[k], recv_sem=st_recv.at[k],
         device_id=(dev,), device_id_type=MESH) for k, dev in enumerate(others)]
-    grad_copies[0].wait_recv()
-    step_scatter(1, 2)
-    head_partial(0)
     for c in stat_copies:
         c.start()
-    step_core(0)
+    grad_copies[0].wait_recv()
     step_gather(1, 2)
+    head_partial(0, between=lambda: step_gather(1, 1))
     step_first(0)
-    step_gather(1, 1)
     step_scatter(0, 0)
     step_gather(1, 0)
     step_scatter(0, 1)
@@ -391,9 +412,9 @@
                 pltpu.VMEM((2, ROWS, EMBED), F32),
                 pltpu.VMEM((TILE_M, ROWS), F32), pltpu.VMEM((TILE_M, ROWS), F32),
                 pltpu.VMEM((TILE_M, ROWS), BF16), pltpu.VMEM((TILE_M, ROWS), BF16),
-                pltpu.VMEM((4, CHUNK_R, ROWS), F32), pltpu.VMEM((16, 4, 8, 128), F32),
+                pltpu.VMEM((4, CHUNK_R, ROWS), F32), pltpu.VMEM((16, 4, 8, 128), F32), pltpu.VMEM((EMBED, EMBED), BF16),
                 dma((2, 3, 9)), dma((2, 3, 9)), dma((9,)), dma((9,)), dma((3,)), dma((3,)), dma((2,)), dma((2,)),
-                dma((6,)), dma((2, 2)), dma((2,)), dma((2,)), dma((2, 3, 3, 2)), dma((2, 3, 3, 2)), dma((2, 3, 3, 2)),
+                dma((7,)), dma((2, 2)), dma((2,)), dma((2,)), dma((2, 3, 3, 2)), dma((2, 3, 3, 2)), dma((2, 3, 3, 2)),
                 dma((2, 3, 3, 2)), dma((2, 4, 3, 2)), dma((2, 4, 3, 2)), dma((15,)), dma((15,)),
                 pltpu.SemaphoreType.REGULAR((2,)),
             ],

time: 247 us -> 240 us (0.972)
  Pallas kernels: 231 us -> 224 us
    pallas_call x1, Pallas kernels: 231 us -> 224 us  [local_fn(): pl.pallas_call(pair_kernel, out_shape=[jax.ShapeDtypeStruct((EMBED, EMBED...]
where the time goes in v5:
time: 240 us
  Pallas kernels  224 us (93%)
  between operations  7.97 us (3%)
  local copies, waits for them, and re-layouts  7.68 us (3%)
    pallas_call x1, Pallas kernels, local_fn(): pl.pallas_call(pair_kernel, out_shape=[jax.ShapeDtypeStruct((EMBED, EMBED...  224 us

profile of v5, /device:TPU:1, one launch (start us, length us, event | category | flops | bytes accessed | tf_op | source)
XLA Modules:
  0.0 240.0 jit_solution(11913627517021202104)
XLA Ops:
  2.0 0.6 pad_maximum_fusion.scal_ref
  2.5 1.7 broadcast_in_dim.2.idrow_ref
  4.2 223.8 %shard_map.110 = (f32[768,768]{1,0:T(8,128)}, f32[768,768]{1,0:T(8,128)}, f32[4,8,128]{2,1,0:T(8,128)}) custom-call(f32[2]{0:T(128)} %pad_maximum_fusion.scal_ref, bf16[1024,768]{1,0:T(8,128)(2,1)} %feat_img.1, bf16[1024,768]{1,0:T(8,128)(2,1)} %feat_txt.1, bf16[768,768]{1,0:T(8,128)(2,1)} %w_img.1, bf16[768,768]{1,0:T(8,128)(2,1)} %w_txt.1, ...), custom_call_target="tpu_custom_call" | custom-call | flops 109999996928 | bytes 16000000 | tf_op jit(solution)/shard_map/pallas_call | solution.py:402
  228.0 1.2 fusion
  231.8 0.0 copy-start
  231.8 3.4 %copy.16 = f32[768,768]{1,0:T(8,128)} copy(f32[768,768]{1,0:T(8,128)} %get-tuple-element.23) | data formatting | bytes 4718592
  235.2 0.0 copy-done
  235.2 1.4 copy.17
Async XLA Ops:
  231.8 3.4 %copy-start = (f32[768,768]{1,0:T(8,128)S(1)}, f32[768,768]{1,0:T(8,128)}, u32[]{:S(2)}) copy-start(f32[768,768]{1,0:T(8,128)} %get-tuple-element.24) | copy-start | bytes 7077892

commit v6 on v5

--- a/solution.py
+++ b/solution.py
@@ -36,7 +36,7 @@
     return [(p, 0 if turn < 0 else turn_rel(turn, p), PART_DIMS[p][k]) for _, k in ways for p in range(3)]
 
 
-def pair_kernel(scal_ref, feat_img, feat_txt, w_img, w_txt, ids_ref, idrow_ref, dw_img_ref, dw_txt_ref, tot_ref,
+def pair_kernel(scal_ref, feat_img, feat_txt, w_img, w_txt, ids_ref, dw_img_ref, dw_txt_ref, tot_ref,
                 slots, ids_raw, ids_all, id_rows, acc, partner, s0, s1, g0, g1, sums, stats, head,
                 send_sem, recv_sem, ids_send, ids_recv, pair_send, pair_recv, grad_send, grad_recv, load_sem,
                 late_sem, core_send, core_recv, rs_send, rs_recv, ag_send, ag_recv, out_send, out_recv, st_send, st_recv, ready):
@@ -57,8 +57,7 @@
     img_loads = [pltpu.make_async_copy(feat_img.at[pl.ds(0, TILE_M)], g0.at[:, pl.ds(0, EMBED)], load_sem.at[2]),
                  pltpu.make_async_copy(feat_img.at[pl.ds(TILE_M, TILE_M)], g1.at[:, pl.ds(0, EMBED)], load_sem.at[3]),
                  pltpu.make_async_copy(w_img, head, load_sem.at[4]),
-                 pltpu.make_async_copy(ids_ref, ids_raw.at[0], load_sem.at[5]),
-                 pltpu.make_async_copy(idrow_ref, id_rows.at[pl.ds(0, ROWS)], load_sem.at[6])]
+                 pltpu.make_async_copy(ids_ref, ids_raw.at[0], load_sem.at[5])]
     for c in txt_loads + img_loads:
         c.start()
     for c in txt_loads:
@@ -112,6 +111,8 @@
         c.wait()
     for c in id_copies:
         c.start()
+    for k in range(0, ROWS, 128):
+        id_rows[k:k + 128, :] = jnp.broadcast_to(ids_raw[0, :, k:k + 128], (128, 128)).T
     slots[1, 0, 0:TILE_M, :] = unit_rows(g0[:, 0:EMBED], head[...])
     slots[1, 0, TILE_M:ROWS, :] = unit_rows(g1[:, 0:EMBED], head[...])
     acc[...] = jnp.zeros_like(acc)
@@ -402,7 +403,7 @@
         dw_img, dw_txt, totals = pl.pallas_call(
             pair_kernel,
             out_shape=[jax.ShapeDtypeStruct((EMBED, EMBED), F32)] * 2 + [jax.ShapeDtypeStruct((4, 8, 128), F32)],
-            in_specs=[smem] + [hbm] * 6,
+            in_specs=[smem] + [hbm] * 5,
             out_specs=[hbm, hbm, vmem],
             scratch_shapes=[
                 pltpu.VMEM((2, 9, ROWS, EMBED), BF16),
@@ -421,8 +422,7 @@
             compiler_params=pltpu.CompilerParams(
                 collective_id=0, has_side_effects=True, vmem_limit_bytes=66_000_000),
             cost_estimate=pl.CostEstimate(flops=110_000_000_000, bytes_accessed=16_000_000, transcendentals=0),
-        )(scal, feat_img, feat_txt, w_img, w_txt, pair_ids.reshape(1, ROWS),
-          jnp.broadcast_to(pair_ids[:, None], (ROWS, 128)))
+        )(scal, feat_img, feat_txt, w_img, w_txt, pair_ids.reshape(1, ROWS))
         loss_sum, temp_sum, bias_sum = totals[0, 0, 0] + totals[1, 0, 0], totals[2, 0, 0], totals[3, 0, 0]
         return loss_sum / total_rows, temp_scale * (temp_sum / total_rows), bias_sum / total_rows, dw_img, dw_txt
 

time: 240 us -> 239 us (level)
  no operation moved by 1% of the time
where the time goes in v6:
time: 239 us; the launch traced here: 238 us
  Pallas kernels  224 us (94%)
  between operations  7.97 us (3%)
  local copies, waits for them, and re-layouts  6 us (3%)
    pallas_call x1, Pallas kernels, local_fn(): pl.pallas_call(pair_kernel, out_shape=[jax.ShapeDtypeStruct((EMBED, EMBED...  224 us
    unnamed x4, local copies, waits for them, and re-layouts  4.78 us

profile of v6, /device:TPU:1, one launch (start us, length us, event | category | flops | bytes accessed | tf_op | source)
XLA Modules:
  0.0 238.2 jit_solution(4849961987772751444)
XLA Ops:
  2.0 0.6 pad_maximum_fusion.scal_ref
  2.5 223.7 %shard_map.110 = (f32[768,768]{1,0:T(8,128)}, f32[768,768]{1,0:T(8,128)}, f32[4,8,128]{2,1,0:T(8,128)}) custom-call(f32[2]{0:T(128)} %pad_maximum_fusion.scal_ref, bf16[1024,768]{1,0:T(8,128)(2,1)} %feat_img.1, bf16[1024,768]{1,0:T(8,128)(2,1)} %feat_txt.1, bf16[768,768]{1,0:T(8,128)(2,1)} %w_img.1, bf16[768,768]{1,0:T(8,128)(2,1)} %w_txt.1, s32[1,1024]{1,0:T(1,128)} %bitcast.7), custom_call_target="tpu_custom_call" | custom-call | flops 109999996928 | bytes 16000000 | tf_op jit(solution)/shard_map/pallas_call | solution.py:403
  226.2 1.2 fusion
  230.1 0.0 copy-start
  230.1 3.4 %copy.16 = f32[768,768]{1,0:T(8,128)} copy(f32[768,768]{1,0:T(8,128)} %get-tuple-element.23) | data formatting | bytes 4718592
  233.4 0.0 copy-done
  233.4 1.4 copy.17
Async XLA Ops:
  230.1 3.4 %copy-start = (f32[768,768]{1,0:T(8,128)S(1)}, f32[768,768]{1,0:T(8,128)}, u32[]{:S(2)}) copy-start(f32[768,768]{1,0:T(8,128)} %get-tuple-element.24) | copy-start | bytes 7077892
